TPU v7x, 256 devices: a whole 4x4x8 slice. The times are simulated.
256 devices in a mesh: gx: 8 (over z), gy: 8 (over x, core), gz: 4 (over y).
Axes of the slice: x: 4, y: 4, z: 8, core: 2. Of those that a mesh axis runs over, the one named last changes fastest.
Arguments:
- displacement: float32 [3, 64, 256, 512], P(None, 'gx', 'gy', 'gz'), may hold values from -0.1 to 0.1
- velocity: float32 [3, 64, 256, 512], P(None, 'gx', 'gy', 'gz'), may hold values from -1.55 to 1.55
- energy: float32 [64, 256, 512], P('gx', 'gy', 'gz'), may hold values from 1 to 4
- density: float32 [64, 256, 512], P('gx', 'gy', 'gz'), may hold values from 0.5 to 4
- region: int32 [64, 256, 512], P('gx', 'gy', 'gz'), may hold values from 0 to 10
- adiabatic: float32 [11], replicated, may hold values from 1.2 to 1.8
- face_flags: int32 [6], replicated, may hold values from 0 to 1
Outputs:
- final_displacement: float32 [3, 64, 256, 512], P(None, 'gx', 'gy', 'gz')
- final_velocity: float32 [3, 64, 256, 512], P(None, 'gx', 'gy', 'gz')
- final_energy: float32 [64, 256, 512], P('gx', 'gy', 'gz')
Inputs may be any that keep to these rules, and one draw needn't show every extreme that they name: `face_flags`: 1 marks a symmetry plane, 0 a free surface.
All inputs are finite; a program needn't handle non-finite values.
Results may differ from a plain program's by a relative error of at most 0.0003.
Values sent between devices are 32-bit elements; how exact they have to be, the bound alone decides.
No kernel may reach another device: no remote copies, remote signals or barrier semaphores. Data moves between devices by JAX's collectives and lax.ppermute only.
A program may use at most 64 MiB of HBM per device.

v0:
```python
import jax
import jax.numpy as jnp
from jax import lax
from jax.sharding import Mesh
from jax.sharding import PartitionSpec as P

STEPS = 2
GY = ("gy_0", "gy_1")
GX_GY_GZ = ("gx", "gy_0", "gy_1", "gz")


COURANT = 0.25
QUAD_COEF = 1.0
LINEAR_COEF = 1.0
CORNERS = [
    (along_x, along_y, along_z) for along_x in (0, 1) for along_y in (0, 1) for along_z in (0, 1)
]


def passed_along(value, axis, steps):
    count = lax.axis_size(axis)
    first, last = (max(0, -steps), min(count, count - steps))
    return lax.ppermute(value, axis, [(source, source + steps) for source in range(first, last)])


def with_halo(array, sides, width):
    edges = {}
    for axis, dim in sides:
        size, length = (lax.axis_size(axis), array.shape[dim])
        up = [(i, (i + 1) % size) for i in range(size - 1)]
        last = lax.slice_in_dim(array, length - width, length, axis=dim)
        first = lax.slice_in_dim(array, 0, width, axis=dim)
        edges[dim] = (
            lax.ppermute(last, axis, up),
            lax.ppermute(first, axis, [(b, a) for a, b in up]),
        )
    done = []
    for _, dim in sides:
        low, high = edges[dim]
        around = [(width, width) if d in done else (0, 0) for d in range(array.ndim)]
        array = jnp.concatenate([jnp.pad(low, around), array, jnp.pad(high, around)], axis=dim)
        done.append(dim)
    return array


def one_axis_at_a_time(array, axes):
    for axis in axes:
        array = lax.pmin(array, axis)
    return array


def corner_views(extended, grid_shape):
    corner_sets = {}
    for offset in CORNERS:
        corner_sets[offset] = extended[
            :,
            offset[0] : offset[0] + grid_shape[0],
            offset[1] : offset[1] + grid_shape[1],
            offset[2] : offset[2] + grid_shape[2],
        ]
    return corner_sets


def spread(corner_sets, start_comp):
    result = []
    for direction in range(3):
        accum = 0.0
        for offset in CORNERS:
            if offset[direction] == 1:
                accum = accum + corner_sets[offset][start_comp : start_comp + 3]
            else:
                accum = accum - corner_sets[offset][start_comp : start_comp + 3]
        result.append(0.25 * accum)
    return result


def cofactors(matrix):

    def minor_det(row_one, row_two, col_one, col_two):
        return (
            matrix[row_one][col_one] * matrix[row_two][col_two]
            - matrix[row_one][col_two] * matrix[row_two][col_one]
        )

    return [
        [minor_det(1, 2, 1, 2), -minor_det(1, 2, 0, 2), minor_det(1, 2, 0, 1)],
        [-minor_det(0, 2, 1, 2), minor_det(0, 2, 0, 2), -minor_det(0, 2, 0, 1)],
        [minor_det(0, 1, 1, 2), -minor_det(0, 1, 0, 2), minor_det(0, 1, 0, 1)],
    ]


def kinematics(corner_sets):
    distorted = spread(corner_sets, 0)
    rate_terms = spread(corner_sets, 3)
    jacobian = [
        [
            distorted[direction][component] + (1.0 if component == direction else 0.0)
            for direction in range(3)
        ]
        for component in range(3)
    ]
    cofactor = cofactors(jacobian)
    volume = (
        jacobian[0][0] * cofactor[0][0]
        + jacobian[0][1] * cofactor[0][1]
        + jacobian[0][2] * cofactor[0][2]
    )
    change = 0.0
    for component in range(3):
        for direction in range(3):
            change = change + cofactor[component][direction] * rate_terms[direction][component]
    return (cofactor, volume, change / volume)


def minmod(forward, backward):
    return jnp.maximum(jnp.minimum(forward, backward), 0.0) + jnp.minimum(
        jnp.maximum(forward, backward), 0.0
    )


def face_ghosts(strain_rate, lower_rate, upper_rate, position, node_count, face_flags, dimension):
    lower_rate = jnp.where(
        position == 0, jnp.where(face_flags[2 * dimension] == 1, strain_rate, 0.0), lower_rate
    )
    upper_rate = jnp.where(
        position == node_count - 2,
        jnp.where(face_flags[2 * dimension + 1] == 1, strain_rate, 0.0),
        upper_rate,
    )
    return (lower_rate, upper_rate)


def stress(strain_rate, roughness, volume, density, energy, gamma_elem, present):
    dense_now = density / volume
    length = jnp.cbrt(volume)
    compress = jnp.maximum(-strain_rate, 0.0)
    viscous = jnp.where(
        present,
        dense_now * length * length * compress * (QUAD_COEF * compress + LINEAR_COEF * roughness),
        0.0,
    )
    pressure = (gamma_elem - 1.0) * dense_now * energy
    sound_sq = gamma_elem * (gamma_elem - 1.0) * energy
    total_stress = jnp.where(present, pressure + viscous, 0.0)
    step_ratio = jnp.where(present, length / jnp.sqrt(sound_sq + viscous / dense_now), jnp.inf)
    return (total_stress, dense_now, step_ratio)


def corner_force(cofactor, total_stress, offset):
    corner_signs = [2.0 * corner_bit - 1.0 for corner_bit in offset]
    return jnp.stack(
        [
            0.25
            * total_stress
            * (
                corner_signs[0] * cofactor[component][0]
                + corner_signs[1] * cofactor[component][1]
                + corner_signs[2] * cofactor[component][2]
            )
            for component in range(3)
        ]
    )


def node_sum(term_of):
    accum = None
    for offset in CORNERS:
        corner_term = term_of(offset)
        padded = jnp.pad(
            corner_term,
            (
                (0, 0),
                (offset[0], 1 - offset[0]),
                (offset[1], 1 - offset[1]),
                (offset[2], 1 - offset[2]),
            ),
        )
        accum = padded if accum is None else accum + padded
    return accum


def apply_walls(speeds, indices, counts, face_flags):
    components = []
    for dimension in range(3):
        on_wall = (indices[dimension] == 0) & (face_flags[2 * dimension] == 1) | (
            indices[dimension] == counts[dimension] - 1
        ) & (face_flags[2 * dimension + 1] == 1)
        components.append(jnp.where(on_wall, 0.0, speeds[dimension]))
    return jnp.stack(components)


def ghost_nodes(fields):
    arrived = passed_along(fields[:, :1], "gx", -1)
    fields = jnp.concatenate([fields, arrived], 1)
    arrived = passed_along(fields[:, :, :1], GY, -1)
    fields = jnp.concatenate([fields, arrived], 2)
    arrived = passed_along(fields[:, :, :, :1], "gz", -1)
    return jnp.concatenate([fields, arrived], 3)


def fold_nodes(partial_value):
    incoming = passed_along(partial_value[:, -1:], "gx", 1)
    partial_value = jnp.concatenate([partial_value[:, :1] + incoming, partial_value[:, 1:-1]], 1)
    incoming = passed_along(partial_value[:, :, -1:], GY, 1)
    partial_value = jnp.concatenate(
        [partial_value[:, :, :1] + incoming, partial_value[:, :, 1:-1]], 2
    )
    incoming = passed_along(partial_value[:, :, :, -1:], "gz", 1)
    return jnp.concatenate([partial_value[:, :, :, :1] + incoming, partial_value[:, :, :, 1:-1]], 3)


def body(displacement, velocity, energy, density, region, adiabatic, face_flags):
    grid_shape = energy.shape
    counts = (
        grid_shape[0] * lax.axis_size("gx"),
        grid_shape[1] * lax.axis_size(GY),
        grid_shape[2] * lax.axis_size("gz"),
    )
    starts = (
        lax.axis_index("gx") * grid_shape[0],
        lax.axis_index(GY) * grid_shape[1],
        lax.axis_index("gz") * grid_shape[2],
    )
    indices = [
        (starts[0] + jnp.arange(grid_shape[0], dtype=jnp.int32))[:, None, None],
        (starts[1] + jnp.arange(grid_shape[1], dtype=jnp.int32))[None, :, None],
        (starts[2] + jnp.arange(grid_shape[2], dtype=jnp.int32))[None, None, :],
    ]
    present = (
        (indices[0] < counts[0] - 1) & (indices[1] < counts[1] - 1) & (indices[2] < counts[2] - 1)
    )
    region_ids = jnp.arange(adiabatic.shape[0], dtype=jnp.int32)[:, None, None, None]
    gamma_elem = jnp.sum(
        jnp.where(region[None] == region_ids, adiabatic[:, None, None, None], 0.0), 0
    )
    mass_term = jnp.where(present, 0.125 * density, 0.0)[None]
    node_mass = None
    for step_index in range(STEPS):
        extended = ghost_nodes(jnp.concatenate([displacement, velocity], 0))
        cofactor, volume, strain_rate = kinematics(corner_views(extended, grid_shape))
        framed = with_halo(strain_rate, (("gx", 0), (GY, 1), ("gz", 2)), 1)
        lowers = [framed[:-2, 1:-1, 1:-1], framed[1:-1, :-2, 1:-1], framed[1:-1, 1:-1, :-2]]
        uppers = [framed[2:, 1:-1, 1:-1], framed[1:-1, 2:, 1:-1], framed[1:-1, 1:-1, 2:]]
        roughness = 0.0
        for dimension in range(3):
            lower_rate, upper_rate = face_ghosts(
                strain_rate,
                lowers[dimension],
                uppers[dimension],
                indices[dimension],
                counts[dimension],
                face_flags,
                dimension,
            )
            roughness = roughness + jnp.abs(
                minmod(upper_rate - strain_rate, strain_rate - lower_rate)
            )
        total_stress, dense_now, step_ratio = stress(
            strain_rate, roughness, volume, density, energy, gamma_elem, present
        )
        time_step = COURANT * one_axis_at_a_time(jnp.min(step_ratio), GX_GY_GZ)
        if node_mass is None:
            node_total = fold_nodes(
                node_sum(
                    lambda offset: jnp.concatenate(
                        [corner_force(cofactor, total_stress, offset), mass_term], 0
                    )
                )
            )
            force = node_total[:3]
            node_mass = node_total[3]
        else:
            force = fold_nodes(
                node_sum(lambda offset: corner_force(cofactor, total_stress, offset))
            )
        velocity = apply_walls(
            velocity + time_step * force / node_mass, indices, counts, face_flags
        )
        displacement = displacement + time_step * velocity
        energy = jnp.where(
            present, energy - time_step * total_stress * strain_rate / dense_now, energy
        )
    return (displacement, velocity, energy)


def solution(mesh):
    torus = Mesh(
        mesh.devices.reshape(mesh.shape["gx"], 4, 2, mesh.shape["gz"]), ("gx", "gy_0", "gy_1", "gz")
    )
    placed = (
        P(None, "gx", GY, "gz"),
        P(None, "gx", GY, "gz"),
        P("gx", GY, "gz"),
        P("gx", GY, "gz"),
        P("gx", GY, "gz"),
        P(),
        P(),
    )
    return jax.shard_map(
        body,
        mesh=torus,
        in_specs=placed,
        out_specs=(P(None, "gx", GY, "gz"), P(None, "gx", GY, "gz"), P("gx", GY, "gz")),
        check_vma=False,
    )
```

profile of v0, /device:TPU:1, one launch (start us, length us, event | category | flops | bytes accessed | tf_op | source)
XLA Modules:
  0.0 220.7 jit_solution(8620764280298421798)
XLA Ops:
  0.7 1.1 constant_dynamic-update-slice_fusion.1
  1.7 1.0 constant_dynamic-update-slice_fusion
  2.8 1.3 collective-permute-start
  4.1 0.7 fusion.116
  5.1 4.0 %collective-permute-done = f32[6,1,32,128]{3,2,1,0:T(8,128)S(1)} collective-permute-done((f32[6,1,32,128]{3,2,1,0:T(8,128)S(1)}, f32[6,1,32,128]{3,2,1,0:T(8,128)S(1)}, u32[]{:S(2)}, u32[]{:S(2)}) %collective-permute-start) | collective-permute-done | bytes 98336 | tf_op jit(solution)/shard_map/ppermute | solution.py:23
  9.2 5.3 %collective-permute-start.1 = (f32[6,9,1,128]{3,2,1,0:T(1,128)S(1)}, f32[6,9,1,128]{3,2,1,0:T(1,128)S(1)}, u32[]{:S(2)}, u32[]{:S(2)}) collective-permute-start(f32[6,9,1,128]{3,2,1,0:T(1,128)S(1)} %pad_maximum_fusion.60), channel_id=1, source_target_pairs={{4,0},{8,4},{12,8},{16,12},{20,16},{24,20},{28,24},{5,1},{9,5},{13... | collective-permute-start | bytes 82952 | tf_op jit(solution)/shard_map/ppermute | solution.py:23
  14.5 1.0 collective-permute-done.1
  16.0 1.3 collective-permute-start.2
  17.3 3.3 %collective-permute-done.2 = f32[6,9,33,1]{2,3,1,0:T(1,128)S(1)} collective-permute-done((f32[6,9,33,1]{2,3,1,0:T(1,128)S(1)}, f32[6,9,33,1]{2,3,1,0:T(1,128)S(1)}, u32[]{:S(2)}, u32[]{:S(2)}) %collective-permute-start.2) | collective-permute-done | bytes 7160 | tf_op jit(solution)/shard_map/ppermute | solution.py:23
  20.6 1.5 copy.43
  22.2 1.5 pad_maximum_fusion
  23.7 0.9 add_multiply_fusion.9
  24.6 0.5 add_multiply_fusion.11
  25.1 0.5 add_multiply_fusion.7
  26.1 3.1 %collective-permute-start.6 = (f32[8,1,128]{2,1,0:T(1,128)S(1)}, f32[8,1,128]{2,1,0:T(1,128)S(1)}, u32[]{:S(2)}, u32[]{:S(2)}) collective-permute-start(f32[8,1,128]{2,1,0:T(1,128)S(1)} %get-tuple-element.153), channel_id=1, source_target_pairs={{0,4},{4,8},{8,12},{12,16},{16,20},{20,24},{24,28},{1,5},{5,9},{9,... | collective-permute-start | bytes 12296 | tf_op jit(solution)/shard_map/ppermute | solution.py:34
  29.2 1.9 collective-permute-start.5
  31.1 3.5 %collective-permute-start.4 = (f32[1,32,128]{2,1,0:T(8,128)S(1)}, f32[1,32,128]{2,1,0:T(8,128)S(1)}, u32[]{:S(2)}, u32[]{:S(2)}) collective-permute-start(f32[1,32,128]{2,1,0:T(8,128)S(1)} %get-tuple-element.155), channel_id=1, source_target_pairs={{0,32},{32,64},{64,96},{96,128},{128,160},{160,192},{192,224},{1,3... | collective-permute-start | bytes 49160 | tf_op jit(solution)/shard_map/ppermute | solution.py:34
  34.7 1.3 collective-permute-start.3
  36.0 1.3 collective-permute-start.7
  37.3 4.0 %collective-permute-start.8 = (f32[8,32,1]{2,1,0:T(8,128)S(1)}, f32[8,32,1]{2,1,0:T(8,128)S(1)}, u32[]{:S(2)}, u32[]{:S(2)}) collective-permute-start(f32[8,32,1]{2,1,0:T(8,128)S(1)} %get-tuple-element.152), channel_id=1, source_target_pairs={{0,1},{1,2},{2,3},{4,5},{5,6},{6,7},{8,9},{9,10},{10,11},{12,13},{... | collective-permute-start | bytes 3080 | tf_op jit(solution)/shard_map/ppermute | solution.py:34
  45.2 1.1 fusion.28
  46.3 16.8 %pmin.56 = f32[]{:T(128)} all-reduce(f32[]{:T(128)} %get-tuple-element.26), channel_id=1, replica_groups=mesh['gx'=8,'gy_0'=4,'gy_1'=2,'gz'=4] {'gx'}, use_global_device_ids=true, to_apply=%region_2.3 | all-reduce | flops 1 | bytes 8 | tf_op jit(solution)/shard_map/pmin | solution.py:48
  63.1 8.0 %pmin.57 = f32[]{:T(128)} all-reduce(f32[]{:T(128)} %pmin.56), channel_id=1, replica_groups=mesh['gx'=8,'gy_0'=4,'gy_1'=2,'gz'=4] {'gy_0'}, use_global_device_ids=true, to_apply=%region_3.4 | all-reduce | flops 1 | bytes 8 | tf_op jit(solution)/shard_map/pmin | solution.py:48
  72.2 1.3 pad_add_fusion
  73.5 2.1 collective-permute-start.9
  75.6 11.3 %pmin.58 = f32[]{:T(128)} all-reduce(f32[]{:T(128)} %pmin.57), channel_id=1, replica_groups=mesh['gx'=8,'gy_0'=4,'gy_1'=2,'gz'=4] {'gy_1'}, use_global_device_ids=true, to_apply=%region_4.5 | all-reduce | flops 1 | bytes 8 | tf_op jit(solution)/shard_map/pmin | solution.py:48
  87.5 1.9 collective-permute-start.10
  90.0 0.6 collective-permute-done.10
  90.8 3.2 %collective-permute-start.11 = (f32[4,8,32,1]{3,2,1,0:T(8,128)S(1)}, f32[4,8,32,1]{3,2,1,0:T(8,128)S(1)}, u32[]{:S(2)}, u32[]{:S(2)}) collective-permute-start(f32[4,8,32,1]{3,2,1,0:T(8,128)S(1)} %fusion.7), channel_id=1, source_target_pairs={{0,1},{1,2},{2,3},{4,5},{5,6},{6,7},{8,9},{9,10},{10,11},{12,13},{... | collective-permute-start | bytes 12296 | tf_op jit(solution)/shard_map/ppermute | solution.py:23
  94.0 16.2 %pmin.59 = f32[]{:T(128)} all-reduce(f32[]{:T(128)} %pmin.58), channel_id=1, replica_groups=mesh['gx'=8,'gy_0'=4,'gy_1'=2,'gz'=4] {'gz'}, use_global_device_ids=true, to_apply=%region_5.6 | all-reduce | flops 1 | bytes 8 | tf_op jit(solution)/shard_map/pmin | solution.py:48
  111.8 1.3 collective-permute-start.12
  113.1 4.1 %collective-permute-done.12 = f32[6,1,32,128]{3,2,1,0:T(8,128)S(1)} collective-permute-done((f32[6,1,32,128]{3,2,1,0:T(8,128)S(1)}, f32[6,1,32,128]{3,2,1,0:T(8,128)S(1)}, u32[]{:S(2)}, u32[]{:S(2)}) %collective-permute-start.12) | collective-permute-done | bytes 98336 | tf_op jit(solution)/shard_map/ppermute | solution.py:23
  117.1 4.9 %collective-permute-start.13 = (f32[6,9,1,128]{3,2,1,0:T(1,128)S(1)}, f32[6,9,1,128]{3,2,1,0:T(1,128)S(1)}, u32[]{:S(2)}, u32[]{:S(2)}) collective-permute-start(f32[6,9,1,128]{3,2,1,0:T(1,128)S(1)} %pad_maximum_fusion.59), channel_id=1, source_target_pairs={{4,0},{8,4},{12,8},{16,12},{20,16},{24,20},{28,24},{5,1},{9,5},{13... | collective-permute-start | bytes 82952 | tf_op jit(solution)/shard_map/ppermute | solution.py:23
  122.1 1.8 collective-permute-done.13
  124.4 1.5 collective-permute-start.14
  125.9 3.5 %collective-permute-done.14 = f32[6,9,33,1]{2,3,1,0:T(1,128)S(1)} collective-permute-done((f32[6,9,33,1]{2,3,1,0:T(1,128)S(1)}, f32[6,9,33,1]{2,3,1,0:T(1,128)S(1)}, u32[]{:S(2)}, u32[]{:S(2)}) %collective-permute-start.14) | collective-permute-done | bytes 7160 | tf_op jit(solution)/shard_map/ppermute | solution.py:23
  129.4 0.5 copy.49
  130.1 0.5 add_multiply_fusion.2
  130.6 0.5 add_multiply_fusion.1
  131.1 0.5 add_multiply_fusion.5
  131.6 0.5 add_multiply_fusion.4
  132.1 0.5 add_multiply_fusion.3
  133.0 2.7 %collective-permute-start.18 = (f32[8,1,128]{2,1,0:T(1,128)S(1)}, f32[8,1,128]{2,1,0:T(1,128)S(1)}, u32[]{:S(2)}, u32[]{:S(2)}) collective-permute-start(f32[8,1,128]{2,1,0:T(1,128)S(1)} %get-tuple-element.124), channel_id=1, source_target_pairs={{0,4},{4,8},{8,12},{12,16},{16,20},{20,24},{24,28},{1,5},{5,9},{9,... | collective-permute-start | bytes 12296 | tf_op jit(solution)/shard_map/ppermute | solution.py:34
  135.8 1.9 collective-permute-start.17
  137.7 3.4 %collective-permute-start.16 = (f32[1,32,128]{2,1,0:T(8,128)S(1)}, f32[1,32,128]{2,1,0:T(8,128)S(1)}, u32[]{:S(2)}, u32[]{:S(2)}) collective-permute-start(f32[1,32,128]{2,1,0:T(8,128)S(1)} %get-tuple-element.126), channel_id=1, source_target_pairs={{0,32},{32,64},{64,96},{96,128},{128,160},{160,192},{192,224},{1,3... | collective-permute-start | bytes 49160 | tf_op jit(solution)/shard_map/ppermute | solution.py:34
  141.1 1.3 collective-permute-start.15
  142.5 1.3 collective-permute-start.19
  143.8 4.0 %collective-permute-start.20 = (f32[8,32,1]{2,1,0:T(8,128)S(1)}, f32[8,32,1]{2,1,0:T(8,128)S(1)}, u32[]{:S(2)}, u32[]{:S(2)}) collective-permute-start(f32[8,32,1]{2,1,0:T(8,128)S(1)} %get-tuple-element.123), channel_id=1, source_target_pairs={{0,1},{1,2},{2,3},{4,5},{5,6},{6,7},{8,9},{9,10},{10,11},{12,13},{... | collective-permute-start | bytes 3080 | tf_op jit(solution)/shard_map/ppermute | solution.py:34
  147.9 1.2 collective-permute-done.19
  149.1 1.8 collective-permute-done.20
  151.0 1.2 fusion.30
  152.2 14.9 %pmin.60 = f32[]{:T(128)} all-reduce(f32[]{:T(128)} %get-tuple-element.8), channel_id=1, replica_groups=mesh['gx'=8,'gy_0'=4,'gy_1'=2,'gz'=4] {'gx'}, use_global_device_ids=true, to_apply=%region_7.8 | all-reduce | flops 1 | bytes 8 | tf_op jit(solution)/shard_map/pmin | solution.py:48
  167.1 6.6 %pmin.61 = f32[]{:T(128)} all-reduce(f32[]{:T(128)} %pmin.60), channel_id=1, replica_groups=mesh['gx'=8,'gy_0'=4,'gy_1'=2,'gz'=4] {'gy_0'}, use_global_device_ids=true, to_apply=%region_8.9 | all-reduce | flops 1 | bytes 8 | tf_op jit(solution)/shard_map/pmin | solution.py:48
  173.7 10.6 %pmin.62 = f32[]{:T(128)} all-reduce(f32[]{:T(128)} %pmin.61), channel_id=1, replica_groups=mesh['gx'=8,'gy_0'=4,'gy_1'=2,'gz'=4] {'gy_1'}, use_global_device_ids=true, to_apply=%region_9.10 | all-reduce | flops 1 | bytes 8 | tf_op jit(solution)/shard_map/pmin | solution.py:48
  184.3 8.8 %pmin.63 = f32[]{:T(128)} all-reduce(f32[]{:T(128)} %pmin.62), channel_id=1, replica_groups=mesh['gx'=8,'gy_0'=4,'gy_1'=2,'gz'=4] {'gz'}, use_global_device_ids=true, to_apply=%region_10.11 | all-reduce | flops 1 | bytes 8 | tf_op jit(solution)/shard_map/pmin | solution.py:48
  193.7 0.8 multiply_bitcast_fusion.23
  194.9 2.8 %fusion = f32[3,9,33,129]{3,2,1,0:T(8,128)S(1)} fusion(f32[1,8,32,128]{3,2,1,0:T(8,128)S(1)} %get-tuple-element.114, f32[1,8,32,128]{3,2,1,0:T(8,128)S(1)} %get-tuple-element.55, f32[1,8,32,128]{3,2,1,0:T(8,128)S(1)} %get-tuple-element.112, f32[1,8,32,128]{3,2,1,0:T(8,128)S(1)} %get-tuple-element.120, f32[1,8,32,128]{3,2,1,0:T(8,128)S(1)} %get-tuple-element.56, ...), kind=kLoop, calls=%fused_computation.18 | loop fusion | flops 12988107 | bytes 3605484 | tf_op jit(solution)/shard_map/add | solution.py:178
  197.8 3.0 %collective-permute-start.21 = (f32[3,1,33,129]{3,2,1,0:T(8,128)S(1)}, f32[3,1,33,129]{3,2,1,0:T(8,128)S(1)}, u32[]{:S(2)}, u32[]{:S(2)}) collective-permute-start(f32[3,1,33,129]{3,2,1,0:T(8,128)S(1)} %slice.720), channel_id=1, source_target_pairs={{0,32},{32,64},{64,96},{96,128},{128,160},{160,192},{192,224},{1,3... | collective-permute-start | bytes 153260 | tf_op jit(solution)/shard_map/ppermute | solution.py:23
  201.2 1.5 collective-permute-done.21
  202.8 4.7 %collective-permute-start.22 = (f32[3,8,1,129]{3,1,2,0:T(8,128)S(1)}, f32[3,8,1,129]{3,1,2,0:T(8,128)S(1)}, u32[]{:S(2)}, u32[]{:S(2)}) collective-permute-start(f32[3,8,1,129]{3,1,2,0:T(8,128)S(1)} %pad_maximum_fusion.61), channel_id=1, source_target_pairs={{0,4},{4,8},{8,12},{12,16},{16,20},{20,24},{24,28},{1,5},{5,9},{9,... | collective-permute-start | bytes 37160 | tf_op jit(solution)/shard_map/ppermute | solution.py:23
  208.6 1.3 collective-permute-start.23
  209.9 8.8 %collective-permute-done.23 = f32[3,8,32,1]{3,2,1,0:T(8,128)S(1)} collective-permute-done((f32[3,8,32,1]{3,2,1,0:T(8,128)S(1)}, f32[3,8,32,1]{3,2,1,0:T(8,128)S(1)}, u32[]{:S(2)}, u32[]{:S(2)}) %collective-permute-start.23) | collective-permute-done | bytes 3104 | tf_op jit(solution)/shard_map/ppermute | solution.py:23
  219.0 0.5 copy-done.19
  219.6 1.0 multiply_add_fusion
  (154 shorter events, 8.1 us)
Async XLA Ops:
  0.6 3.5 %copy-start.17 = (s32[6]{0:T(128)S(1)}, s32[6]{0:T(128)}, u32[]{:S(2)}) copy-start(s32[6]{0:T(128)} %param.13) | copy-start | bytes 76
  0.6 4.2 %copy-start.36 = (f32[11]{0:T(128)S(1)}, f32[11]{0:T(128)}, u32[]{:S(2)}) copy-start(f32[11]{0:T(128)} %param.12) | copy-start | bytes 136
  0.7 4.2 %copy-start.16 = (s32[8,32,128]{2,1,0:T(8,128)S(1)}, s32[8,32,128]{2,1,0:T(8,128)}, u32[]{:S(2)}) copy-start(s32[8,32,128]{2,1,0:T(8,128)} %param.11) | copy-start | bytes 393220
  2.8 6.4 %collective-permute-start = (f32[6,1,32,128]{3,2,1,0:T(8,128)S(1)}, f32[6,1,32,128]{3,2,1,0:T(8,128)S(1)}, u32[]{:S(2)}, u32[]{:S(2)}) collective-permute-start(f32[6,1,32,128]{3,2,1,0:T(8,128)S(1)} %slice.632), channel_id=1, source_target_pairs={{32,0},{64,32},{96,64},{128,96},{160,128},{192,160},{224,192},{33,... | collective-permute-start | bytes 294920 | tf_op jit(solution)/shard_map/ppermute | solution.py:23
  5.1 66.0 %copy-start.4 = (f32[8,32,128]{2,1,0:T(8,128)}, f32[8,32,128]{2,1,0:T(8,128)S(1)}, u32[]{:S(2)}) copy-start(f32[8,32,128]{2,1,0:T(8,128)S(1)} %select_reduce_fusion) | copy-start | bytes 393220
  5.1 40.0 %copy-start.24 = (pred[8]{0:T(512)(128)(4,1)}, pred[8]{0:T(512)(128)(4,1)S(1)}, u32[]{:S(2)}) copy-start(pred[8]{0:T(512)(128)(4,1)S(1)} %get-tuple-element.167) | copy-start | bytes 28
  5.1 40.0 %copy-start.26 = (pred[8]{0:T(512)(128)(4,1)}, pred[8]{0:T(512)(128)(4,1)S(1)}, u32[]{:S(2)}) copy-start(pred[8]{0:T(512)(128)(4,1)S(1)} %get-tuple-element.168) | copy-start | bytes 28
  9.2 6.3 %collective-permute-start.1 = (f32[6,9,1,128]{3,2,1,0:T(1,128)S(1)}, f32[6,9,1,128]{3,2,1,0:T(1,128)S(1)}, u32[]{:S(2)}, u32[]{:S(2)}) collective-permute-start(f32[6,9,1,128]{3,2,1,0:T(1,128)S(1)} %pad_maximum_fusion.60), channel_id=1, source_target_pairs={{4,0},{8,4},{12,8},{16,12},{20,16},{24,20},{28,24},{5,1},{9,5},{13... | collective-permute-start | bytes 82952 | tf_op jit(solution)/shard_map/ppermute | solution.py:23
  14.4 30.7 %copy-start.28 = (pred[32]{0:T(512)(128)(4,1)}, pred[32]{0:T(512)(128)(4,1)S(1)}, u32[]{:S(2)}) copy-start(pred[32]{0:T(512)(128)(4,1)S(1)} %get-tuple-element.165) | copy-start | bytes 100
  14.5 30.7 %copy-start.30 = (pred[32]{0:T(512)(128)(4,1)}, pred[32]{0:T(512)(128)(4,1)S(1)}, u32[]{:S(2)}) copy-start(pred[32]{0:T(512)(128)(4,1)S(1)} %get-tuple-element.166) | copy-start | bytes 100
  16.0 4.6 %collective-permute-start.2 = (f32[6,9,33,1]{2,3,1,0:T(1,128)S(1)}, f32[6,9,33,1]{2,3,1,0:T(1,128)S(1)}, u32[]{:S(2)}, u32[]{:S(2)}) collective-permute-start(f32[6,9,33,1]{2,3,1,0:T(1,128)S(1)} %copy.54), channel_id=1, source_target_pairs={{1,0},{2,1},{3,2},{5,4},{6,5},{7,6},{9,8},{10,9},{11,10},{13,12},{... | collective-permute-start | bytes 21392 | tf_op jit(solution)/shard_map/ppermute | solution.py:23
  17.3 27.8 %copy-start.32 = (pred[128]{0:T(512)(128)(4,1)}, pred[128]{0:T(512)(128)(4,1)S(1)}, u32[]{:S(2)}) copy-start(pred[128]{0:T(512)(128)(4,1)S(1)} %get-tuple-element.163) | copy-start | bytes 388
  17.3 27.8 %copy-start.34 = (pred[128]{0:T(512)(128)(4,1)}, pred[128]{0:T(512)(128)(4,1)S(1)}, u32[]{:S(2)}) copy-start(pred[128]{0:T(512)(128)(4,1)S(1)} %get-tuple-element.164) | copy-start | bytes 388
  22.2 1.5 copy-start
  22.2 1.5 copy-start.1
  25.6 19.5 %copy-start.6 = (f32[8,32,128]{2,1,0:T(8,128)S(1)}, f32[8,32,128]{2,1,0:T(8,128)}, u32[]{:S(2)}) copy-start(f32[8,32,128]{2,1,0:T(8,128)} %param.10) | copy-start | bytes 393220
  25.6 19.5 %copy-start.10 = (f32[8,32,128]{2,1,0:T(8,128)S(1)}, f32[8,32,128]{2,1,0:T(8,128)}, u32[]{:S(2)}) copy-start(f32[8,32,128]{2,1,0:T(8,128)} %param.9) | copy-start | bytes 393220
  26.0 19.2 %copy-start.2 = (f32[8,32,128]{2,1,0:T(8,128)}, f32[8,32,128]{2,1,0:T(8,128)S(1)}, u32[]{:S(2)}) copy-start(f32[8,32,128]{2,1,0:T(8,128)S(1)} %get-tuple-element.30) | copy-start | bytes 393220
  26.0 45.3 %copy-start.8 = (f32[8,32,128]{2,1,0:T(8,128)}, f32[8,32,128]{2,1,0:T(8,128)S(1)}, u32[]{:S(2)}) copy-start(f32[8,32,128]{2,1,0:T(8,128)S(1)} %get-tuple-element.37) | copy-start | bytes 393220
  26.1 11.2 %collective-permute-start.6 = (f32[8,1,128]{2,1,0:T(1,128)S(1)}, f32[8,1,128]{2,1,0:T(1,128)S(1)}, u32[]{:S(2)}, u32[]{:S(2)}) collective-permute-start(f32[8,1,128]{2,1,0:T(1,128)S(1)} %get-tuple-element.153), channel_id=1, source_target_pairs={{0,4},{4,8},{8,12},{12,16},{16,20},{20,24},{24,28},{1,5},{5,9},{9,... | collective-permute-start | bytes 12296 | tf_op jit(solution)/shard_map/ppermute | solution.py:34
  29.2 15.8 %collective-permute-start.5 = (f32[8,1,128]{2,1,0:T(1,128)S(1)}, f32[8,1,128]{2,1,0:T(1,128)S(1)}, u32[]{:S(2)}, u32[]{:S(2)}) collective-permute-start(f32[8,1,128]{2,1,0:T(1,128)S(1)} %get-tuple-element.154), channel_id=1, source_target_pairs={{4,0},{8,4},{12,8},{16,12},{20,16},{24,20},{28,24},{5,1},{9,5},{13... | collective-permute-start | bytes 12296 | tf_op jit(solution)/shard_map/ppermute | solution.py:35
  31.1 14.0 %collective-permute-start.4 = (f32[1,32,128]{2,1,0:T(8,128)S(1)}, f32[1,32,128]{2,1,0:T(8,128)S(1)}, u32[]{:S(2)}, u32[]{:S(2)}) collective-permute-start(f32[1,32,128]{2,1,0:T(8,128)S(1)} %get-tuple-element.155), channel_id=1, source_target_pairs={{0,32},{32,64},{64,96},{96,128},{128,160},{160,192},{192,224},{1,3... | collective-permute-start | bytes 49160 | tf_op jit(solution)/shard_map/ppermute | solution.py:34
  34.7 10.4 %collective-permute-start.3 = (f32[1,32,128]{2,1,0:T(8,128)S(1)}, f32[1,32,128]{2,1,0:T(8,128)S(1)}, u32[]{:S(2)}, u32[]{:S(2)}) collective-permute-start(f32[1,32,128]{2,1,0:T(8,128)S(1)} %get-tuple-element.156), channel_id=1, source_target_pairs={{32,0},{64,32},{96,64},{128,96},{160,128},{192,160},{224,192},{33,... | collective-permute-start | bytes 49160 | tf_op jit(solution)/shard_map/ppermute | solution.py:35
  36.0 9.1 %collective-permute-start.7 = (f32[8,32,1]{2,1,0:T(8,128)S(1)}, f32[8,32,1]{2,1,0:T(8,128)S(1)}, u32[]{:S(2)}, u32[]{:S(2)}) collective-permute-start(f32[8,32,1]{2,1,0:T(8,128)S(1)} %get-tuple-element.151), channel_id=1, source_target_pairs={{1,0},{2,1},{3,2},{5,4},{6,5},{7,6},{9,8},{10,9},{11,10},{13,12},{... | collective-permute-start | bytes 3080 | tf_op jit(solution)/shard_map/ppermute | solution.py:35
  37.3 7.8 %collective-permute-start.8 = (f32[8,32,1]{2,1,0:T(8,128)S(1)}, f32[8,32,1]{2,1,0:T(8,128)S(1)}, u32[]{:S(2)}, u32[]{:S(2)}) collective-permute-start(f32[8,32,1]{2,1,0:T(8,128)S(1)} %get-tuple-element.152), channel_id=1, source_target_pairs={{0,1},{1,2},{2,3},{4,5},{5,6},{6,7},{8,9},{9,10},{10,11},{12,13},{... | collective-permute-start | bytes 3080 | tf_op jit(solution)/shard_map/ppermute | solution.py:34
  46.3 25.4 %copy-start.12 = (f32[8,32,128]{2,1,0:T(8,128)}, f32[8,32,128]{2,1,0:T(8,128)S(1)}, u32[]{:S(2)}) copy-start(f32[8,32,128]{2,1,0:T(8,128)S(1)} %get-tuple-element.27) | copy-start | bytes 393220
  63.1 48.1 %copy-start.18 = (pred[8]{0:T(512)(128)(4,1)}, pred[8]{0:T(512)(128)(4,1)S(1)}, u32[]{:S(2)}) copy-start(pred[8]{0:T(512)(128)(4,1)S(1)} %and_or_fusion.2) | copy-start | bytes 28
  73.5 13.8 %collective-permute-start.9 = (f32[4,1,33,129]{3,2,1,0:T(8,128)S(1)}, f32[4,1,33,129]{3,2,1,0:T(8,128)S(1)}, u32[]{:S(2)}, u32[]{:S(2)}) collective-permute-start(f32[4,1,33,129]{3,2,1,0:T(8,128)S(1)} %slice.671), channel_id=1, source_target_pairs={{0,32},{32,64},{64,96},{96,128},{128,160},{160,192},{192,224},{1,3... | collective-permute-start | bytes 204344 | tf_op jit(solution)/shard_map/ppermute | solution.py:23
  75.6 35.6 %copy-start.20 = (pred[32]{0:T(512)(128)(4,1)}, pred[32]{0:T(512)(128)(4,1)S(1)}, u32[]{:S(2)}) copy-start(pred[32]{0:T(512)(128)(4,1)S(1)} %and_or_fusion.1) | copy-start | bytes 100
  87.5 3.1 %collective-permute-start.10 = (f32[4,8,1,129]{3,1,2,0:T(8,128)S(1)}, f32[4,8,1,129]{3,1,2,0:T(8,128)S(1)}, u32[]{:S(2)}, u32[]{:S(2)}) collective-permute-start(f32[4,8,1,129]{3,1,2,0:T(8,128)S(1)} %pad_maximum_fusion.58), channel_id=1, source_target_pairs={{0,4},{4,8},{8,12},{12,16},{16,20},{20,24},{24,28},{1,5},{5,9},{9,... | collective-permute-start | bytes 49544 | tf_op jit(solution)/shard_map/ppermute | solution.py:23
  90.8 20.1 %collective-permute-start.11 = (f32[4,8,32,1]{3,2,1,0:T(8,128)S(1)}, f32[4,8,32,1]{3,2,1,0:T(8,128)S(1)}, u32[]{:S(2)}, u32[]{:S(2)}) collective-permute-start(f32[4,8,32,1]{3,2,1,0:T(8,128)S(1)} %fusion.7), channel_id=1, source_target_pairs={{0,1},{1,2},{2,3},{4,5},{5,6},{6,7},{8,9},{9,10},{10,11},{12,13},{... | collective-permute-start | bytes 12296 | tf_op jit(solution)/shard_map/ppermute | solution.py:23
  94.0 17.2 %copy-start.22 = (pred[128]{0:T(512)(128)(4,1)}, pred[128]{0:T(512)(128)(4,1)S(1)}, u32[]{:S(2)}) copy-start(pred[128]{0:T(512)(128)(4,1)S(1)} %and_or_fusion) | copy-start | bytes 388
  111.1 0.7 copy-start.14
  111.8 5.4 %collective-permute-start.12 = (f32[6,1,32,128]{3,2,1,0:T(8,128)S(1)}, f32[6,1,32,128]{3,2,1,0:T(8,128)S(1)}, u32[]{:S(2)}, u32[]{:S(2)}) collective-permute-start(f32[6,1,32,128]{3,2,1,0:T(8,128)S(1)} %pad_maximum_fusion.55), channel_id=1, source_target_pairs={{32,0},{64,32},{96,64},{128,96},{160,128},{192,160},{224,192},{33,... | collective-permute-start | bytes 294920 | tf_op jit(solution)/shard_map/ppermute | solution.py:23
  117.1 6.7 %collective-permute-start.13 = (f32[6,9,1,128]{3,2,1,0:T(1,128)S(1)}, f32[6,9,1,128]{3,2,1,0:T(1,128)S(1)}, u32[]{:S(2)}, u32[]{:S(2)}) collective-permute-start(f32[6,9,1,128]{3,2,1,0:T(1,128)S(1)} %pad_maximum_fusion.59), channel_id=1, source_target_pairs={{4,0},{8,4},{12,8},{16,12},{20,16},{24,20},{28,24},{5,1},{9,5},{13... | collective-permute-start | bytes 82952 | tf_op jit(solution)/shard_map/ppermute | solution.py:23
  124.4 5.0 %collective-permute-start.14 = (f32[6,9,33,1]{2,3,1,0:T(1,128)S(1)}, f32[6,9,33,1]{2,3,1,0:T(1,128)S(1)}, u32[]{:S(2)}, u32[]{:S(2)}) collective-permute-start(f32[6,9,33,1]{2,3,1,0:T(1,128)S(1)} %copy.55), channel_id=1, source_target_pairs={{1,0},{2,1},{3,2},{5,4},{6,5},{7,6},{9,8},{10,9},{11,10},{13,12},{... | collective-permute-start | bytes 21392 | tf_op jit(solution)/shard_map/ppermute | solution.py:23
  132.6 18.3 %copy-start.3 = (f32[8,32,128]{2,1,0:T(8,128)S(1)}, f32[8,32,128]{2,1,0:T(8,128)}, u32[]{:S(2)}) copy-start(f32[8,32,128]{2,1,0:T(8,128)} %copy-done.2) | copy-start | bytes 393220
  132.6 18.3 %copy-start.5 = (f32[8,32,128]{2,1,0:T(8,128)S(1)}, f32[8,32,128]{2,1,0:T(8,128)}, u32[]{:S(2)}) copy-start(f32[8,32,128]{2,1,0:T(8,128)} %copy-done.4) | copy-start | bytes 393220
  132.6 18.3 %copy-start.7 = (f32[8,32,128]{2,1,0:T(8,128)S(1)}, f32[8,32,128]{2,1,0:T(8,128)}, u32[]{:S(2)}) copy-start(f32[8,32,128]{2,1,0:T(8,128)} %param.10) | copy-start | bytes 393220
  132.6 18.3 %copy-start.9 = (f32[8,32,128]{2,1,0:T(8,128)S(1)}, f32[8,32,128]{2,1,0:T(8,128)}, u32[]{:S(2)}) copy-start(f32[8,32,128]{2,1,0:T(8,128)} %copy-done.8) | copy-start | bytes 393220
  132.6 18.3 %copy-start.11 = (f32[8,32,128]{2,1,0:T(8,128)S(1)}, f32[8,32,128]{2,1,0:T(8,128)}, u32[]{:S(2)}) copy-start(f32[8,32,128]{2,1,0:T(8,128)} %param.9) | copy-start | bytes 393220
  132.6 18.3 %copy-start.13 = (f32[8,32,128]{2,1,0:T(8,128)S(1)}, f32[8,32,128]{2,1,0:T(8,128)}, u32[]{:S(2)}) copy-start(f32[8,32,128]{2,1,0:T(8,128)} %copy-done.12) | copy-start | bytes 393220
  132.6 18.3 %copy-start.25 = (pred[8]{0:T(512)(128)(4,1)S(1)}, pred[8]{0:T(512)(128)(4,1)}, u32[]{:S(2)}) copy-start(pred[8]{0:T(512)(128)(4,1)} %copy-done.24) | copy-start | bytes 28
  132.6 18.3 %copy-start.27 = (pred[8]{0:T(512)(128)(4,1)S(1)}, pred[8]{0:T(512)(128)(4,1)}, u32[]{:S(2)}) copy-start(pred[8]{0:T(512)(128)(4,1)} %copy-done.26) | copy-start | bytes 28
  132.7 18.3 %copy-start.29 = (pred[32]{0:T(512)(128)(4,1)S(1)}, pred[32]{0:T(512)(128)(4,1)}, u32[]{:S(2)}) copy-start(pred[32]{0:T(512)(128)(4,1)} %copy-done.28) | copy-start | bytes 100
  132.7 18.3 %copy-start.31 = (pred[32]{0:T(512)(128)(4,1)S(1)}, pred[32]{0:T(512)(128)(4,1)}, u32[]{:S(2)}) copy-start(pred[32]{0:T(512)(128)(4,1)} %copy-done.30) | copy-start | bytes 100
  132.7 18.3 %copy-start.33 = (pred[128]{0:T(512)(128)(4,1)S(1)}, pred[128]{0:T(512)(128)(4,1)}, u32[]{:S(2)}) copy-start(pred[128]{0:T(512)(128)(4,1)} %copy-done.32) | copy-start | bytes 388
  132.7 18.3 %copy-start.35 = (pred[128]{0:T(512)(128)(4,1)S(1)}, pred[128]{0:T(512)(128)(4,1)}, u32[]{:S(2)}) copy-start(pred[128]{0:T(512)(128)(4,1)} %copy-done.34) | copy-start | bytes 388
  133.0 10.8 %collective-permute-start.18 = (f32[8,1,128]{2,1,0:T(1,128)S(1)}, f32[8,1,128]{2,1,0:T(1,128)S(1)}, u32[]{:S(2)}, u32[]{:S(2)}) collective-permute-start(f32[8,1,128]{2,1,0:T(1,128)S(1)} %get-tuple-element.124), channel_id=1, source_target_pairs={{0,4},{4,8},{8,12},{12,16},{16,20},{20,24},{24,28},{1,5},{5,9},{9,... | collective-permute-start | bytes 12296 | tf_op jit(solution)/shard_map/ppermute | solution.py:34
  135.8 12.1 %collective-permute-start.17 = (f32[8,1,128]{2,1,0:T(1,128)S(1)}, f32[8,1,128]{2,1,0:T(1,128)S(1)}, u32[]{:S(2)}, u32[]{:S(2)}) collective-permute-start(f32[8,1,128]{2,1,0:T(1,128)S(1)} %get-tuple-element.125), channel_id=1, source_target_pairs={{4,0},{8,4},{12,8},{16,12},{20,16},{24,20},{28,24},{5,1},{9,5},{13... | collective-permute-start | bytes 12296 | tf_op jit(solution)/shard_map/ppermute | solution.py:35
  137.7 13.2 %collective-permute-start.16 = (f32[1,32,128]{2,1,0:T(8,128)S(1)}, f32[1,32,128]{2,1,0:T(8,128)S(1)}, u32[]{:S(2)}, u32[]{:S(2)}) collective-permute-start(f32[1,32,128]{2,1,0:T(8,128)S(1)} %get-tuple-element.126), channel_id=1, source_target_pairs={{0,32},{32,64},{64,96},{96,128},{128,160},{160,192},{192,224},{1,3... | collective-permute-start | bytes 49160 | tf_op jit(solution)/shard_map/ppermute | solution.py:34
  141.1 9.7 %collective-permute-start.15 = (f32[1,32,128]{2,1,0:T(8,128)S(1)}, f32[1,32,128]{2,1,0:T(8,128)S(1)}, u32[]{:S(2)}, u32[]{:S(2)}) collective-permute-start(f32[1,32,128]{2,1,0:T(8,128)S(1)} %get-tuple-element.127), channel_id=1, source_target_pairs={{32,0},{64,32},{96,64},{128,96},{160,128},{192,160},{224,192},{33,... | collective-permute-start | bytes 49160 | tf_op jit(solution)/shard_map/ppermute | solution.py:35
  142.5 6.6 %collective-permute-start.19 = (f32[8,32,1]{2,1,0:T(8,128)S(1)}, f32[8,32,1]{2,1,0:T(8,128)S(1)}, u32[]{:S(2)}, u32[]{:S(2)}) collective-permute-start(f32[8,32,1]{2,1,0:T(8,128)S(1)} %get-tuple-element.122), channel_id=1, source_target_pairs={{1,0},{2,1},{3,2},{5,4},{6,5},{7,6},{9,8},{10,9},{11,10},{13,12},{... | collective-permute-start | bytes 3080 | tf_op jit(solution)/shard_map/ppermute | solution.py:35
  143.8 7.0 %collective-permute-start.20 = (f32[8,32,1]{2,1,0:T(8,128)S(1)}, f32[8,32,1]{2,1,0:T(8,128)S(1)}, u32[]{:S(2)}, u32[]{:S(2)}) collective-permute-start(f32[8,32,1]{2,1,0:T(8,128)S(1)} %get-tuple-element.123), channel_id=1, source_target_pairs={{0,1},{1,2},{2,3},{4,5},{5,6},{6,7},{8,9},{9,10},{10,11},{12,13},{... | collective-permute-start | bytes 3080 | tf_op jit(solution)/shard_map/ppermute | solution.py:34
  197.8 4.9 %collective-permute-start.21 = (f32[3,1,33,129]{3,2,1,0:T(8,128)S(1)}, f32[3,1,33,129]{3,2,1,0:T(8,128)S(1)}, u32[]{:S(2)}, u32[]{:S(2)}) collective-permute-start(f32[3,1,33,129]{3,2,1,0:T(8,128)S(1)} %slice.720), channel_id=1, source_target_pairs={{0,32},{32,64},{64,96},{96,128},{128,160},{160,192},{192,224},{1,3... | collective-permute-start | bytes 153260 | tf_op jit(solution)/shard_map/ppermute | solution.py:23
  202.8 5.7 %collective-permute-start.22 = (f32[3,8,1,129]{3,1,2,0:T(8,128)S(1)}, f32[3,8,1,129]{3,1,2,0:T(8,128)S(1)}, u32[]{:S(2)}, u32[]{:S(2)}) collective-permute-start(f32[3,8,1,129]{3,1,2,0:T(8,128)S(1)} %pad_maximum_fusion.61), channel_id=1, source_target_pairs={{0,4},{4,8},{8,12},{12,16},{16,20},{20,24},{24,28},{1,5},{5,9},{9,... | collective-permute-start | bytes 37160 | tf_op jit(solution)/shard_map/ppermute | solution.py:23
  208.5 10.3 %copy-start.15 = (f32[8,32,128]{2,1,0:T(8,128)S(1)}, f32[8,32,128]{2,1,0:T(8,128)}, u32[]{:S(2)}) copy-start(f32[8,32,128]{2,1,0:T(8,128)} %copy-done.14) | copy-start | bytes 393220
  208.6 10.2 %collective-permute-start.23 = (f32[3,8,32,1]{3,2,1,0:T(8,128)S(1)}, f32[3,8,32,1]{3,2,1,0:T(8,128)S(1)}, u32[]{:S(2)}, u32[]{:S(2)}) collective-permute-start(f32[3,8,32,1]{3,2,1,0:T(8,128)S(1)} %fusion.11), channel_id=1, source_target_pairs={{0,1},{1,2},{2,3},{4,5},{5,6},{6,7},{8,9},{9,10},{10,11},{12,13},{... | collective-permute-start | bytes 9224 | tf_op jit(solution)/shard_map/ppermute | solution.py:23
  218.9 0.7 copy-start.19
  218.9 0.7 copy-start.21
  218.9 0.7 copy-start.23
where the time goes:
time: 222 us; the launch traced here: 221 us
  blocking collectives  93.1 us (42%)
  starting transfers between devices  61.6 us (28%)
  waiting for transfers between devices  32 us (14%)
  other arithmetic  18.3 us (8%)
  local copies, waits for them, and re-layouts  8.71 us (4%)
  between operations  6.94 us (3%)
    pmin x8, blocking collectives, one_axis_at_a_time(): array = lax.pmin(array, axis)  93.1 us
    ppermute x12, starting transfers between devices, passed_along(): lax.ppermute(value, axis, [(source, source + steps) for source in range(f...  31.8 us
    ppermute x12, waiting for transfers between devices, passed_along(): lax.ppermute(value, axis, [(source, source + steps) for source in range(f...  29 us
    ppermute x6, starting transfers between devices, with_halo(): lax.ppermute(last, axis, up)  20.7 us
    ppermute x6, starting transfers between devices, with_halo(): lax.ppermute(first, axis, [(b, a) for a, b in up])  9.01 us
  transfers between devices with their start and end apart: 24, of which 12 were waited for; matrix products, arithmetic and copies ran while one was open for 1% of the time, Pallas kernels for 0%

commit v1 on v0

v1 whole, which is shorter than its diff:
```python
import functools

import jax
import jax.numpy as jnp
from jax import lax
from jax.experimental import pallas as pl
from jax.experimental.pallas import tpu as pltpu
from jax.sharding import Mesh
from jax.sharding import PartitionSpec as P

GY = ("gy_0", "gy_1")
AXES = ("gx", "gy_0", "gy_1", "gz")

BX, BY, BZ = 8, 32, 128
PX = BX + 4
EX = BX + 1
ROWS = BY + 8
GROUPS = ROWS // 8
LANES = 2 * BZ
SLABS = 6 * PX + 3 * EX
PACKED = -(-SLABS * GROUPS // 32)
FAR = 1 << 20
MIB = 1 << 20


def next_z(v):
    return pltpu.roll(v, LANES - 1, 1)


def prev_z(v):
    return pltpu.roll(v, 1, 1)


def next_row(v):
    return pltpu.roll(v, 7, 0)


def prev_row(v):
    return pltpu.roll(v, 1, 0)


def slab_ids():
    for field in range(6):
        for plane in range(PX):
            yield field * PX + plane, field, plane
    for field in range(6, 9):
        for plane in range(EX):
            yield 6 * PX + (field - 6) * EX + plane, field, plane


def pack_x(gamma_table, disp, vel, energy, density, region, up, down, gamma):
    for field in range(6):
        src = disp if field < 3 else vel
        for p in range(2):
            up[2 * field + p] = src[field % 3, BX - 2 + p]
            down[2 * field + p] = src[field % 3, p]
    ids = region[...]
    value = jnp.zeros(ids.shape, jnp.float32)
    for r in range(gamma_table.shape[0]):
        value = jnp.where(ids == r, gamma_table[r], value)
    gamma[...] = value
    up[12] = energy[BX - 1]
    up[13] = density[BX - 1]
    up[14] = value[BX - 1]


def slab_source(field, plane, disp, vel, energy, density, gamma, x_low, x_high):
    if field < 6:
        if plane < 2:
            return x_low, (2 * field + plane,)
        if plane < BX + 2:
            return (disp if field < 3 else vel), (field % 3, plane - 2)
        return x_high, (2 * field + plane - BX - 2,)
    if plane == 0:
        return x_low, (12 + field - 6,)
    return (energy, density, gamma)[field - 6], (plane - 1,)


def pack_y(disp, vel, energy, density, gamma, x_low, x_high, up, down):
    for k, field, plane in slab_ids():
        ref, at = slab_source(field, plane, disp, vel, energy, density, gamma, x_low, x_high)
        up[4 * k : 4 * k + 4] = ref[(*at, slice(BY - 4, BY))]
        down[4 * k : 4 * k + 4] = ref[(*at, slice(0, 4))]


def pack_z(disp, vel, energy, density, gamma, x_low, x_high, y_low, y_high, main, up, down, stage):
    quad = lax.broadcasted_iota(jnp.int32, (8, BZ), 1) // 4
    for k, field, plane in slab_ids():
        ref, at = slab_source(field, plane, disp, vel, energy, density, gamma, x_low, x_high)
        stage[k, 0:4] = y_low[4 * k : 4 * k + 4]
        stage[k, 4 : BY + 4] = ref[(*at, slice(0, BY))]
        stage[k, BY + 4 : BY + 8] = y_high[4 * k : 4 * k + 4]
    for slot in range(PACKED):
        to_up = jnp.zeros((8, BZ), jnp.float32)
        to_down = jnp.zeros((8, BZ), jnp.float32)
        for q in range(32):
            n = 32 * slot + q
            if n >= SLABS * GROUPS:
                break
            k, j = divmod(n, GROUPS)
            value = stage[k, pl.ds(j, 8, stride=GROUPS), :]
            main[k, j] = value
            to_up = jnp.where(quad == q, pltpu.roll(value, (4 * q + 4) % BZ, 1), to_up)
            here = pltpu.roll(value, 4 * q, 1) if q else value
            to_down = jnp.where(quad == q, here, to_down)
        up[8 * slot : 8 * slot + 8] = to_up
        down[8 * slot : 8 * slot + 8] = to_down


class Place:
    def __init__(self, where):
        self.x0, self.y0, self.z0 = where[0], where[1], where[2]
        self.nx, self.ny, self.nz = where[3], where[4], where[5]
        self.flag = [where[6 + i] for i in range(6)]
        sublane = lax.broadcasted_iota(jnp.int32, (8, LANES), 0)
        lane = lax.broadcasted_iota(jnp.int32, (8, LANES), 1)
        self.row = GROUPS * sublane + (self.y0 - 4)
        self.col = jnp.where(lane < LANES - BZ // 2, lane, lane - LANES) + self.z0
        inside = (self.col >= 0) & (self.col < self.nz - 1)
        self.row_inside = jnp.where(inside, self.row, -FAR)

    def present(self, plane, j):
        x = self.x0 + plane
        ok = (x >= 0) & (x < self.nx - 1)
        top = jnp.where(ok, self.ny - 1 - j, -2 * FAR)
        return (self.row_inside >= -j) & (self.row_inside < top)

    def counted(self, plane, j):
        x = self.x0 + plane
        ok = (x >= 0) & (x < self.nx - 1)
        top = jnp.where(ok, jnp.minimum(self.ny - 1, self.y0 + BY) - j, -2 * FAR)
        rows = self.row_inside[:, :BZ]
        return (rows >= self.y0 - j) & (rows < top)


def open_factor(flag):
    return jnp.where(flag == 1, 0.0, 1.0)


def strain_pass(place, fs, fd, cof, vol, inv, strain):
    def plane_step(x, carry):
        for j in range(GROUPS):
            grad = []
            for f in range(6):
                a, b = fs[f, x, j], fs[f, x + 1, j]
                c, d = fs[f, x, j + 1], fs[f, x + 1, j + 1]
                p, q = d - a, b - c
                gz = (fd[f, x, j] + fd[f, x + 1, j]) + (fd[f, x, j + 1] + fd[f, x + 1, j + 1])
                grad.append([p + q, p - q, gz])
            m = [[grad[d][e] + 4.0 if d == e else grad[d][e] for e in range(3)] for d in range(3)]
            g = grad[3:]

            def minor(r, s, u, w):
                return m[r][u] * m[s][w] - m[r][w] * m[s][u]

            c = [
                [minor(1, 2, 1, 2), minor(1, 2, 2, 0), minor(1, 2, 0, 1)],
                [minor(2, 0, 1, 2), minor(2, 0, 2, 0), minor(2, 0, 0, 1)],
                [minor(0, 1, 1, 2), minor(0, 1, 2, 0), minor(0, 1, 0, 1)],
            ]
            volume = m[0][0] * c[0][0] + m[0][1] * c[0][1] + m[0][2] * c[0][2]
            change = c[0][0] * g[0][0]
            for d in range(3):
                for e in range(3):
                    if d or e:
                        change = change + c[d][e] * g[d][e]
                    cof[3 * d + e, x, j] = c[d][e]
            inverse = 1.0 / volume
            rate = change * inverse
            vol[x, j] = volume
            inv[x, j] = inverse
            strain[x, j + 1] = rate
            if j == 0:
                strain[x, GROUPS + 1] = next_row(rate)
            if j == GROUPS - 1:
                strain[x, 0] = prev_row(rate)
        return carry

    lax.fori_loop(0, PX - 1, plane_step, 0)


def limited(forward, backward):
    return jnp.maximum(jnp.minimum(forward, backward), 0.0) - jnp.minimum(
        jnp.maximum(forward, backward), 0.0
    )


def stress_pass(place, cof, vol, inv, strain, energy, density, gamma, terms, work, least):
    opened = [open_factor(f) for f in place.flag]

    def plane_step(i, low):
        x = i + 1
        gx = place.x0 + i - 1
        for j in range(GROUPS):
            s = strain[x, j + 1]
            back = jnp.where(gx == 0, s * opened[0], s - strain[x - 1, j + 1])
            fore = jnp.where(gx == place.nx - 2, -s * opened[1], strain[x + 1, j + 1] - s)
            rough = limited(fore, back)
            back = jnp.where(place.row == -j, s * opened[2], s - strain[x, j])
            fore = jnp.where(
                place.row == place.ny - 2 - j, -s * opened[3], strain[x, j + 2] - s
            )
            rough = rough + limited(fore, back)
            back = jnp.where(place.col == 0, s * opened[4], s - prev_z(s))
            fore = jnp.where(place.col == place.nz - 2, -s * opened[5], next_z(s) - s)
            rough = rough + limited(fore, back)
            volume = vol[x, j]
            root = jnp.exp(jnp.log(jnp.abs(volume)) * (1.0 / 3.0))
            root = jnp.where(volume < 0.0, -root, root)
            compress = jnp.maximum(-s, 0.0)
            quad = (root * root) * (0.0625 * compress) * (compress + rough)
            g, e = gamma[i, j], energy[i, j]
            base = (g - 1.0) * e
            both = base + quad
            ratio = root[:, :BZ] * lax.rsqrt(g[:, :BZ] * base[:, :BZ] + quad[:, :BZ])
            low = jnp.minimum(low, jnp.where(place.counted(i - 1, j), ratio, jnp.inf))
            work[i, j] = s * both
            t = jnp.where(place.present(i - 1, j), density[i, j] * inv[x, j] * both, 0.0)
            for d in range(3):
                t0, t1, t2 = t * cof[3 * d, x, j], t * cof[3 * d + 1, x, j], t * cof[3 * d + 2, x, j]
                for n, value in enumerate((t0 + t1, t0 - t1, t2)):
                    terms[3 * d + n, i, j + 1] = value
                    if j == GROUPS - 1:
                        terms[3 * d + n, i, 0] = prev_row(value)
        return low

    low = lax.fori_loop(0, EX, plane_step, jnp.full((8, BZ), jnp.inf, jnp.float32))
    low = jnp.broadcast_to(jnp.min(low, axis=0, keepdims=True), (8, BZ))
    for r in range(0, least.shape[0], 8):
        least[r : r + 8] = low


def force_of(terms, d, x, j):
    m, n, t = 3 * d, 3 * d + 1, 3 * d + 2
    r = terms[m, x, j] - terms[n, x + 1, j] + terms[n, x, j + 1] - terms[m, x + 1, j + 1]
    q = (terms[t, x, j] + terms[t, x + 1, j]) + (terms[t, x, j + 1] + terms[t, x + 1, j + 1])
    return (r - q) + prev_z(r + q)


def first_step(
    where, main, z_low, z_high,
    fs_d, fd_d, vel, energy, density, gamma, terms, work, least,
    fs, fd, cof, vol, inv, strain,
):
    place = Place(where)
    lane = lax.broadcasted_iota(jnp.int32, (8, BZ), 1)

    def extended(k, j):
        slot, q = divmod(k * GROUPS + j, 32)
        high = z_high[8 * slot : 8 * slot + 8]
        high = pltpu.roll(high, BZ - 4 * q, 1) if q else high
        low = z_low[8 * slot : 8 * slot + 8]
        low = pltpu.roll(low, BZ - 4 - 4 * q, 1) if q < 31 else low
        return jnp.concatenate([main[k, j], jnp.where(lane < BZ // 2, high, low)], axis=1)

    for k, field, plane in slab_ids():
        for j in range(GROUPS):
            value = extended(k, j)
            if field < 6:
                after = next_z(value)
                both, gap = value + after, after - value
                for out, v in ((fs, both), (fd, gap)):
                    out[field, plane, j] = v
                    if j == 0:
                        out[field, plane, GROUPS] = next_row(v)
                if field < 3:
                    fs_d[field, plane, j] = both
                    fd_d[field, plane, j] = gap
                else:
                    vel[field - 3, plane, j] = value
            else:
                (energy, density, gamma)[field - 6][plane, j] = value
    strain_pass(place, fs, fd, cof, vol, inv, strain)
    stress_pass(place, cof, vol, inv, strain, energy, density, gamma, terms, work, least)


def first_push(where, density, terms, accel_low, accel_mid, accel_high, unmass, held):
    place = Place(where)
    for i in range(EX):
        for j in range(GROUPS):
            value = jnp.where(place.present(i - 1, j), density[i, j], 0.0)
            held[i, j + 1] = value
            if j == GROUPS - 1:
                held[i, 0] = prev_row(value)
    for x in range(BX):
        for j in range(GROUPS):
            mass = (held[x, j] + held[x + 1, j]) + (held[x, j + 1] + held[x + 1, j + 1])
            mass = 0.125 * (mass + prev_z(mass))
            some = mass > 0.0
            recip = jnp.where(some, 1.0 / jnp.where(some, mass, 1.0), 0.0)
            unmass[x, j] = recip[:, :BZ]
            for d in range(3):
                value = force_of(terms, d, x, j) * recip
                if x < 2:
                    accel_low[d, x, j] = value
                elif x < BX - 2:
                    accel_mid[d, x - 2, j] = value
                else:
                    accel_high[d, x - BX + 2, j] = value


def least_of(ref):
    return jnp.min(ref[...])


def second_step(
    where, lows, fs_d, fd_d, vel, energy, density, gamma, work,
    got_low, accel_low, accel_mid, accel_high, got_high,
    new_vel, new_energy, terms, new_work, least,
    fs, fd, cof, vol, inv, strain, moved,
):
    place = Place(where)
    dt = least_of(lows) * 0.0625
    wall = [jnp.where(place.flag[2 * d] == 1, 0, -FAR) for d in range(3)]
    last = (place.nx - 1, place.ny - 1, place.nz - 1)
    edge = [jnp.where(place.flag[2 * d + 1] == 1, last[d], -FAR) for d in range(3)]
    on_z = (place.col == wall[2]) | (place.col == edge[2])
    for x in range(PX):
        gx = place.x0 + x - 2
        on_x = (gx == wall[0]) | (gx == edge[0])
        for j in range(GROUPS):
            for d in range(3):
                if x < 2:
                    push = got_low[d, x, j]
                elif x < 4:
                    push = accel_low[d, x - 2, j]
                elif x < BX:
                    push = accel_mid[d, x - 4, j]
                elif x < BX + 2:
                    push = accel_high[d, x - BX, j]
                else:
                    push = got_high[d, x - BX - 2, j]
                v = vel[d, x, j] + dt * push
                if d == 0:
                    v = jnp.where(on_x, 0.0, v)
                elif d == 1:
                    v = jnp.where((place.row == wall[1] - j) | (place.row == edge[1] - j), 0.0, v)
                else:
                    v = jnp.where(on_z, 0.0, v)
                if 2 <= x < BX + 2:
                    new_vel[d, x - 2, j] = v[:, :BZ]
                after = next_z(v)
                both, gap = v + after, after - v
                for out, old, u in ((fs, fs_d, both), (fd, fd_d, gap)):
                    w = old[d, x, j] + dt * u
                    out[d, x, j] = w
                    out[d + 3, x, j] = u
                    if j == 0:
                        out[d, x, GROUPS] = next_row(w)
                        out[d + 3, x, GROUPS] = next_row(u)
    for i in range(EX):
        for j in range(GROUPS):
            e = energy[i, j]
            e = jnp.where(place.present(i - 1, j), e - dt * work[i, j], e)
            moved[i, j] = e
            if i:
                new_energy[i - 1, j] = e[:, :BZ]
    strain_pass(place, fs, fd, cof, vol, inv, strain)
    stress_pass(place, cof, vol, inv, strain, moved, density, gamma, terms, new_work, least)


def second_push(
    terms, unmass, new_vel, new_energy, new_work,
    out_accel, out_vel, out_energy, out_work, stage,
):
    for x in range(BX):
        for j in range(GROUPS):
            rows = pl.ds(j, 8, stride=GROUPS)
            for d in range(3):
                stage[x, d, rows, :] = force_of(terms, d, x, j)[:, :BZ] * unmass[x, j]
                stage[x, 3 + d, rows, :] = new_vel[d, x, j]
            stage[x, 6, rows, :] = new_energy[x, j]
            stage[x, 7, rows, :] = new_work[x + 1, j, :, :BZ]
        for d in range(3):
            out_accel[d, x] = stage[x, d, 4 : BY + 4, :]
            out_vel[d, x] = stage[x, 3 + d, 4 : BY + 4, :]
        out_energy[x] = stage[x, 6, 4 : BY + 4, :]
        out_work[x] = stage[x, 7, 4 : BY + 4, :]


def finish(where, lows, again, disp, vel, accel, energy, work, new_disp, new_vel, new_energy):
    dt = least_of(lows) * 0.0625
    dt2 = least_of(again) * 0.0625
    x0, y0, z0 = where[0], where[1], where[2]
    nx, ny, nz = where[3], where[4], where[5]
    row = lax.broadcasted_iota(jnp.int32, (BY, BZ), 0) + y0
    col = lax.broadcasted_iota(jnp.int32, (BY, BZ), 1) + z0

    def walled(at, low, high, count):
        return ((at == 0) & (where[low] == 1)) | ((at == count - 1) & (where[high] == 1))

    on_y, on_z = walled(row, 8, 9, ny), walled(col, 10, 11, nz)
    inside = (row < ny - 1) & (col < nz - 1)
    for x in range(BX):
        on_x = walled(x0 + x, 6, 7, nx)
        for d in range(3):
            v = vel[d, x]
            u = jnp.where((on_x, on_y, on_z)[d], 0.0, v + dt2 * accel[d, x])
            new_vel[d, x] = u
            new_disp[d, x] = (disp[d, x] + dt * v) + dt2 * u
        e = energy[x]
        moved = jnp.where(inside, e - dt2 * work[x], e)
        new_energy[x] = jnp.where(x0 + x < nx - 1, moved, e)


def call(kernel, outs, args, smem=0, scratch=(), limit=48):
    specs = [
        pl.BlockSpec(memory_space=pltpu.SMEM if i < smem else pltpu.VMEM) for i in range(len(args))
    ]
    return pl.pallas_call(
        kernel,
        out_shape=[jax.ShapeDtypeStruct(s, jnp.float32) for s in outs],
        in_specs=specs,
        out_specs=[pl.BlockSpec(memory_space=pltpu.VMEM) for _ in outs],
        scratch_shapes=[pltpu.VMEM(s, jnp.float32) for s in scratch],
        compiler_params=pltpu.CompilerParams(vmem_limit_bytes=limit * MIB),
        name=kernel.__name__,
    )(*args)


def swap(up, down, axis):
    size = lax.axis_size(axis)
    ring = [(i, (i + 1) % size) for i in range(size)]
    low = lax.ppermute(up, axis, ring)
    high = lax.ppermute(down, axis, [(b, a) for a, b in ring])
    return low, high


def body(displacement, velocity, energy, density, region, adiabatic, face_flags):
    assert energy.shape == (BX, BY, BZ)
    sizes = (lax.axis_size("gx"), lax.axis_size(GY), lax.axis_size("gz"))
    devices = sizes[0] * sizes[1] * sizes[2]
    where = jnp.stack(
        [
            lax.axis_index("gx") * BX,
            lax.axis_index(GY) * BY,
            lax.axis_index("gz") * BZ,
            jnp.int32(sizes[0] * BX),
            jnp.int32(sizes[1] * BY),
            jnp.int32(sizes[2] * BZ),
        ]
    )
    where = jnp.concatenate([where, face_flags])
    block = (BX, BY, BZ)
    up, down, gamma = call(
        pack_x,
        [(15, BY, BZ), (12, BY, BZ), block],
        (adiabatic, displacement, velocity, energy, density, region),
        smem=1,
        limit=8,
    )
    x_low, x_high = swap(up, down, "gx")
    own = (displacement, velocity, energy, density, gamma, x_low, x_high)
    up, down = call(pack_y, [(4 * SLABS, BZ)] * 2, own, limit=8)
    y_low, y_high = swap(up, down, GY)
    main, up, down = call(
        pack_z,
        [(SLABS, GROUPS, 8, BZ), (8 * PACKED, BZ), (8 * PACKED, BZ)],
        (*own, y_low, y_high),
        scratch=[(SLABS, ROWS, BZ)],
        limit=16,
    )
    z_low, z_high = swap(up, down, "gz")

    chunk = (GROUPS, 8, LANES)
    slots = (GROUPS + 1, 8, LANES)
    passes = [
        (6, PX, *slots),
        (6, PX, *slots),
        (9, PX - 1, *chunk),
        (PX - 1, *chunk),
        (PX - 1, *chunk),
        (PX - 1, GROUPS + 2, 8, LANES),
    ]
    fs_d, fd_d, vel, e, rho, g, terms, work, least = call(
        first_step,
        [(3, PX, *chunk)] * 3 + [(EX, *chunk)] * 3 + [(9, EX, *slots), (EX, *chunk), (devices, BZ)],
        (where, main, z_low, z_high),
        smem=1,
        scratch=passes,
        limit=36,
    )
    lows = lax.all_to_all(least, AXES, 0, 0, tiled=True)
    a_low, a_mid, a_high, unmass = call(
        first_push,
        [(3, 2, *chunk), (3, BX - 4, *chunk), (3, 2, *chunk), (BX, GROUPS, 8, BZ)],
        (where, rho, terms),
        smem=1,
        scratch=[(EX, *slots)],
        limit=16,
    )
    got_low, got_high = swap(a_high, a_low, "gx")
    new_vel, new_e, terms, work, least = call(
        second_step,
        [(3, BX, GROUPS, 8, BZ), (BX, GROUPS, 8, BZ), (9, EX, *slots), (EX, *chunk), (devices, BZ)],
        (where, lows, fs_d, fd_d, vel, e, rho, g, work, got_low, a_low, a_mid, a_high, got_high),
        smem=1,
        scratch=[*passes, (EX, *chunk)],
        limit=36,
    )
    again = lax.all_to_all(least, AXES, 0, 0, tiled=True)
    accel, vel, e, work = call(
        second_push,
        [(3, *block), (3, *block), block, block],
        (terms, unmass, new_vel, new_e, work),
        scratch=[(BX, 8, ROWS, BZ)],
        limit=16,
    )
    return tuple(
        call(
            finish,
            [(3, *block), (3, *block), block],
            (where, lows, again, displacement, vel, accel, e, work),
            smem=1,
            limit=12,
        )
    )


def solution(mesh):
    torus = Mesh(
        mesh.devices.reshape(mesh.shape["gx"], mesh.shape["gy"] // 2, 2, mesh.shape["gz"]), AXES
    )
    nodes, elements = P(None, "gx", GY, "gz"), P("gx", GY, "gz")
    return jax.shard_map(
        body,
        mesh=torus,
        in_specs=(nodes, nodes, elements, elements, elements, P(), P()),
        out_specs=(nodes, nodes, elements),
        check_vma=False,
    )
```

time: 222 us -> 149 us (0.67)
  blocking collectives: 93.1 us -> 0 us
  local copies, waits for them, and re-layouts: 8.71 us -> 45.8 us
  Pallas kernels: 0 us -> 37 us
  starting transfers between devices: 61.6 us -> 41 us
  other arithmetic: 18.3 us -> 0 us
  waiting for transfers between devices: 32 us -> 23 us
  between operations: 6.94 us -> 0.82 us
    pmin x8 -> x0, blocking collectives: 93.1 us -> none  [one_axis_at_a_time(): array = lax.pmin(array, axis)]
    ppermute x24 -> x8, starting transfers between devices: 61.6 us -> 16.1 us  [the longest x4 8.39 us: swap(): high = lax.ppermute(down, axis, [(b, a) for a, b in ring])]
    unnamed x77 -> x106, local copies, waits for them, and re-layouts: 3.04 us -> 45.7 us
    pallas_call x0 -> x8, Pallas kernels: none -> 37 us  [call(): pl.pallas_call(kernel, out_shape=[jax.ShapeDtypeStruct(s, jnp.float32) fo...]
    all_to_all x0 -> x2, starting transfers between devices: none -> 24.8 us  [the longest x1 13.3 us: body(): again = lax.all_to_all(least, AXES, 0, 0, tiled=True)]
    ppermute x24 -> x8, waiting for transfers between devices: 32 us -> 16.8 us  [the longest x4 10.8 us: swap(): low = lax.ppermute(up, axis, ring)]
    all_to_all x0 -> x2, waiting for transfers between devices: none -> 6.21 us  [the longest x1 6.21 us: body(): again = lax.all_to_all(least, AXES, 0, 0, tiled=True)]
    add x12 -> x0, other arithmetic: 5.66 us -> none  [the longest x2 4.12 us: node_sum(): accum = padded if accum is None else accum + padded]
  transfers between devices with their start and end apart: 24 -> 10, of which waited for: 12 -> 7; matrix products, arithmetic and copies ran while one was open for 1% -> 0% of each run, Pallas kernels for 0% -> 1%
where the time goes in v1:
time: 149 us; the launch traced here: 148 us
  local copies, waits for them, and re-layouts  45.8 us (31%)
  starting transfers between devices  41 us (28%)
  Pallas kernels  37 us (25%)
  waiting for transfers between devices  23 us (15%)
    unnamed x106, local copies, waits for them, and re-layouts  45.7 us
    pallas_call x8, Pallas kernels, call(): pl.pallas_call(kernel, out_shape=[jax.ShapeDtypeStruct(s, jnp.float32) fo...  37 us
    all_to_all x1, starting transfers between devices, body(): again = lax.all_to_all(least, AXES, 0, 0, tiled=True)  13.3 us
    all_to_all x1, starting transfers between devices, body(): lows = lax.all_to_all(least, AXES, 0, 0, tiled=True)  11.5 us
    ppermute x4, waiting for transfers between devices, swap(): low = lax.ppermute(up, axis, ring)  10.8 us
    ppermute x4, starting transfers between devices, swap(): high = lax.ppermute(down, axis, [(b, a) for a, b in ring])  8.39 us
    ppermute x4, starting transfers between devices, swap(): low = lax.ppermute(up, axis, ring)  7.74 us
    all_to_all x1, waiting for transfers between devices, body(): again = lax.all_to_all(least, AXES, 0, 0, tiled=True)  6.21 us
  transfers between devices with their start and end apart: 10, of which 7 were waited for; matrix products, arithmetic and copies ran while one was open for 0% of the time, Pallas kernels for 1%

profile of v1, /device:TPU:1, one launch (start us, length us, event | category | flops | bytes accessed | tf_op | source)
XLA Modules:
  0.0 147.7 jit_solution(4012602782538347343)
XLA Ops:
  0.6 1.0 copy-done
  1.6 1.0 copy-done.7
  2.6 0.9 copy-done.19
  3.5 0.9 copy-done.22
  4.4 0.9 copy-done.49
  6.0 0.7 pack_x.1
  6.7 2.5 %collective-permute-start = (f32[15,32,128]{2,1,0:T(8,128)S(1)}, f32[15,32,128]{2,1,0:T(8,128)S(1)}, u32[]{:S(2)}, u32[]{:S(2)}) collective-permute-start(f32[15,32,128]{2,1,0:T(8,128)S(1)} %get-tuple-element.34), channel_id=1, source_target_pairs={{0,32},{32,64},{64,96},{96,128},{128,160},{160,192},{192,224},{224... | collective-permute-start | bytes 737288 | tf_op jit(solution)/shard_map/ppermute | solution.py:424
  9.2 4.0 %collective-permute-start.1 = (f32[12,32,128]{2,1,0:T(8,128)S(1)}, f32[12,32,128]{2,1,0:T(8,128)S(1)}, u32[]{:S(2)}, u32[]{:S(2)}) collective-permute-start(f32[12,32,128]{2,1,0:T(8,128)S(1)} %get-tuple-element.35), channel_id=1, source_target_pairs={{32,0},{64,32},{96,64},{128,96},{160,128},{192,160},{224,192},{0,2... | collective-permute-start | bytes 589832 | tf_op jit(solution)/shard_map/ppermute | solution.py:425
  13.3 3.6 %collective-permute-done.1.x_high = f32[12,32,128]{2,1,0:T(8,128)S(1)} collective-permute-done((f32[12,32,128]{2,1,0:T(8,128)S(1)}, f32[12,32,128]{2,1,0:T(8,128)S(1)}, u32[]{:S(2)}, u32[]{:S(2)}) %collective-permute-start.1) | collective-permute-done | bytes 196640 | tf_op jit(solution)/shard_map/ppermute | solution.py:425
  16.8 2.0 %collective-permute-done.x_low = f32[15,32,128]{2,1,0:T(8,128)S(1)} collective-permute-done((f32[15,32,128]{2,1,0:T(8,128)S(1)}, f32[15,32,128]{2,1,0:T(8,128)S(1)}, u32[]{:S(2)}, u32[]{:S(2)}) %collective-permute-start) | collective-permute-done | bytes 245792 | tf_op jit(solution)/shard_map/ppermute | solution.py:424
  18.8 1.0 copy-done.1
  19.8 1.0 copy-done.8
  20.8 0.9 copy-done.20
  21.7 0.9 copy-done.23
  22.7 2.4 %collective-permute-start.2 = (f32[396,128]{1,0:T(8,128)S(1)}, f32[396,128]{1,0:T(8,128)S(1)}, u32[]{:S(2)}, u32[]{:S(2)}) collective-permute-start(f32[396,128]{1,0:T(8,128)S(1)} %get-tuple-element.36), channel_id=1, source_target_pairs={{0,4},{4,8},{8,12},{12,16},{16,20},{20,24},{24,28},{28,0},{1,5},{5... | collective-permute-start | bytes 608264 | tf_op jit(solution)/shard_map/ppermute | solution.py:424
  25.1 2.7 %collective-permute-done.2.y_low = f32[396,128]{1,0:T(8,128)S(1)} collective-permute-done((f32[396,128]{1,0:T(8,128)S(1)}, f32[396,128]{1,0:T(8,128)S(1)}, u32[]{:S(2)}, u32[]{:S(2)}) %collective-permute-start.2) | collective-permute-done | bytes 202784 | tf_op jit(solution)/shard_map/ppermute | solution.py:424
  27.8 2.5 %collective-permute-done.3.y_high = f32[396,128]{1,0:T(8,128)S(1)} collective-permute-done((f32[396,128]{1,0:T(8,128)S(1)}, f32[396,128]{1,0:T(8,128)S(1)}, u32[]{:S(2)}, u32[]{:S(2)}) %collective-permute-start.3) | collective-permute-done | bytes 202784 | tf_op jit(solution)/shard_map/ppermute | solution.py:425
  30.3 1.2 pack_z.1
  31.5 1.4 collective-permute-start.4
  32.9 1.5 %collective-permute-start.5 = (f32[128,128]{1,0:T(8,128)S(1)}, f32[128,128]{1,0:T(8,128)S(1)}, u32[]{:S(2)}, u32[]{:S(2)}) collective-permute-start(f32[128,128]{1,0:T(8,128)S(1)} %get-tuple-element.40), channel_id=1, source_target_pairs={{1,0},{2,1},{3,2},{0,3},{5,4},{6,5},{7,6},{4,7},{9,8},{10,9},{11,1... | collective-permute-start | bytes 196616 | tf_op jit(solution)/shard_map/ppermute | solution.py:425
  34.5 2.0 %collective-permute-done.4.z_low = f32[128,128]{1,0:T(8,128)S(1)} collective-permute-done((f32[128,128]{1,0:T(8,128)S(1)}, f32[128,128]{1,0:T(8,128)S(1)}, u32[]{:S(2)}, u32[]{:S(2)}) %collective-permute-start.4) | collective-permute-done | bytes 65568 | tf_op jit(solution)/shard_map/ppermute | solution.py:424
  36.4 27.7 %first_step.1 = (f32[3,12,5,8,256]{4,3,2,1,0:T(8,128)S(1)}, f32[3,12,5,8,256]{4,3,2,1,0:T(8,128)S(1)}, f32[3,12,5,8,256]{4,3,2,1,0:T(8,128)S(1)}, f32[9,5,8,256]...) custom-call(s32[12]{0:T(128)S(1)} %concatenate.3.where, ...), custom_call_target="tpu_custom_call" | custom-call | tf_op jit(solution)/shard_map/first_step/pallas_call | solution.py:410
  64.1 1.9 %copy-done.5 = f32[9,9,6,8,256]{4,3,2,1,0:T(8,128)} copy-done((f32[9,9,6,8,256]{4,3,2,1,0:T(8,128)}, f32[9,9,6,8,256]{4,3,2,1,0:T(8,128)S(1)}, u32[]{:S(2)}) %copy-start.5) | copy-done | bytes 3981336
  66.1 1.2 copy-done.10
  67.2 1.1 copy-done.12
  68.4 1.2 copy-done.14
  69.6 0.7 copy-done.16
  70.3 0.7 copy-done.31
  71.0 0.7 copy-done.33
  71.8 0.7 copy-done.35
  72.5 11.5 %all-to-all-start = ((f32[256,1,128]{2,1,0:T(1,128)}), f32[256,1,128]{2,1,0:T(1,128)S(1)}, u32[]{:S(2)}, u32[]{:S(2)}) async-start(f32[256,1,128]{2,1,0:T(1,128)} %bitcast.4), calls=%async_computation | async-start | bytes 262144 | tf_op jit(solution)/shard_map/all_to_all | solution.py:483
  84.0 2.1 %copy-done.6 = f32[9,9,6,8,256]{4,3,2,1,0:T(8,128)S(1)} copy-done((f32[9,9,6,8,256]{4,3,2,1,0:T(8,128)S(1)}, f32[9,9,6,8,256]{4,3,2,1,0:T(8,128)}, u32[]{:S(2)}) %copy-start.6) | copy-done | bytes 3981336
  86.1 1.0 copy-done.17
  87.1 1.1 first_push.1
  88.2 0.8 copy-done.25
  89.7 1.5 %collective-permute-start.6 = (f32[3,2,5,8,256]{4,3,2,1,0:T(8,128)S(1)}, f32[3,2,5,8,256]{4,3,2,1,0:T(8,128)S(1)}, u32[]{:S(2)}, u32[]{:S(2)}) collective-permute-start(f32[3,2,5,8,256]{4,3,2,1,0:T(8,128)S(1)} %get-tuple-element.50.accel_high), channel_id=1, source_target_pairs={{0,32},{32,64},{64,96},{96,128},{128,160},{160,192},{192,224},{224... | collective-permute-start | bytes 737288 | tf_op jit(solution)/shard_map/ppermute | solution.py:424
  91.1 0.7 copy-done.39
  91.8 2.8 %collective-permute-start.7 = (f32[3,2,5,8,256]{4,3,2,1,0:T(8,128)S(1)}, f32[3,2,5,8,256]{4,3,2,1,0:T(8,128)S(1)}, u32[]{:S(2)}, u32[]{:S(2)}) collective-permute-start(f32[3,2,5,8,256]{4,3,2,1,0:T(8,128)S(1)} %get-tuple-element.51.accel_low), channel_id=1, source_target_pairs={{32,0},{64,32},{96,64},{128,96},{160,128},{192,160},{224,192},{0,2... | collective-permute-start | bytes 737288 | tf_op jit(solution)/shard_map/ppermute | solution.py:425
  94.7 0.7 copy-done.37
  95.4 4.1 %collective-permute-done.6.got_low = f32[3,2,5,8,256]{4,3,2,1,0:T(8,128)S(1)} collective-permute-done((f32[3,2,5,8,256]{4,3,2,1,0:T(8,128)S(1)}, f32[3,2,5,8,256]{4,3,2,1,0:T(8,128)S(1)}, u32[]{:S(2)}, u32[]{:S(2)}) %collective-permute-start.6) | collective-permute-done | bytes 245792 | tf_op jit(solution)/shard_map/ppermute | solution.py:424
  99.5 0.7 copy-done.41
  100.2 0.7 copy-done.43
  100.9 1.4 copy-done.15
  102.3 1.0 copy-done.18
  103.3 1.0 copy-done.26
  104.3 1.0 copy-done.32
  105.3 1.0 copy-done.34
  106.3 1.0 copy-done.36
  107.3 0.9 copy-done.38
  108.2 0.9 copy-done.40
  109.2 0.9 copy-done.42
  110.1 0.9 copy-done.44
  111.1 4.2 %second_step.1 = (f32[3,8,5,8,128]{4,3,2,1,0:T(8,128)S(1)}, f32[8,5,8,128]{3,2,1,0:T(8,128)S(1)}, f32[9,9,6,8,256]{4,3,2,1,0:T(8,128)S(1)}, f32[9,5,8,256]{3,2,1,0:T(8,128)S(1)}, f32[256,128]{1,0:T(8,128)S(1)}) custom-call(s32[12]{0:T(128)S(1)} %concatenate.3.where, f32[256,128]{1,0:T(8,128)S(1)} %bitcast.11, f32[3,12,5,8,256]{4,3,2,1,0:T(8,128)S(1)} %copy-done.11, ...), custom_call_target="tpu_custom_call" | custom-call | tf_op jit(solution)/shard_map/second_step/pallas_call | solution.py:410
  115.3 1.9 %copy-done.3 = f32[9,9,6,8,256]{4,3,2,1,0:T(8,128)} copy-done((f32[9,9,6,8,256]{4,3,2,1,0:T(8,128)}, f32[9,9,6,8,256]{4,3,2,1,0:T(8,128)S(1)}, u32[]{:S(2)}) %copy-start.3) | copy-done | bytes 3981336
  117.2 0.8 copy-done.27
  118.0 0.7 copy-done.29
  120.0 13.3 %all-to-all-start.1 = ((f32[256,1,128]{2,1,0:T(1,128)}), f32[256,1,128]{2,1,0:T(1,128)S(1)}, u32[]{:S(2)}, u32[]{:S(2)}) async-start(f32[256,1,128]{2,1,0:T(1,128)} %bitcast.14), calls=%async_computation.1 | async-start | bytes 262144 | tf_op jit(solution)/shard_map/all_to_all | solution.py:501
  133.4 2.1 %copy-done.4 = f32[9,9,6,8,256]{4,3,2,1,0:T(8,128)S(1)} copy-done((f32[9,9,6,8,256]{4,3,2,1,0:T(8,128)S(1)}, f32[9,9,6,8,256]{4,3,2,1,0:T(8,128)}, u32[]{:S(2)}) %copy-start.4) | copy-done | bytes 3981336
  135.5 1.0 copy-done.28
  136.5 1.0 copy-done.30
  137.5 0.9 copy-done.46
  138.4 0.9 copy-done.48
  139.8 6.2 %all-to-all-done.1 = f32[256,1,128]{2,1,0:T(1,128)S(1)} async-done(((f32[256,1,128]{2,1,0:T(1,128)}), f32[256,1,128]{2,1,0:T(1,128)S(1)}, u32[]{:S(2)}, u32[]{:S(2)}) %all-to-all-start.1) | async-done | bytes 131104 | tf_op jit(solution)/shard_map/all_to_all | solution.py:501
  146.0 1.6 %finish.1 = (f32[3,8,32,128]{3,2,1,0:T(8,128)}, f32[3,8,32,128]{3,2,1,0:T(8,128)}, f32[8,32,128]{2,1,0:T(8,128)}) custom-call(s32[12]{0:T(128)S(1)} %concatenate.3.where, f32[256,128]{1,0:T(8,128)S(1)} %bitcast.12, f32[256,128]{1,0:T(8,128)S(1)} %bitcast.13, f32[3,8,32,128]{3,2,1,0:T(8,128)S(1)} %copy-done.2, f32[3,8,32,128]{3,2,1,0:T(8,128)S(1)} %get-tuple-element.59.vel, ...), custom_call_target="tpu_custom_call" | custom-call | tf_op jit(solution)/shard_map/finish/pallas_call | solution.py:410
  (71 shorter events, 3.4 us)
Async XLA Ops:
  0.6 1.0 copy-start
  1.6 1.0 copy-start.7
  2.6 0.9 copy-start.19
  3.5 0.9 copy-start.22
  4.4 0.9 copy-start.49
  5.3 0.7 copy-start.51
  6.0 24.2 %copy-start.2 = (f32[3,8,32,128]{3,2,1,0:T(8,128)S(1)}, f32[3,8,32,128]{3,2,1,0:T(8,128)}, u32[]{:S(2)}) copy-start(f32[3,8,32,128]{3,2,1,0:T(8,128)} %disp.7) | copy-start | bytes 1179652
  6.0 24.2 %copy-start.9 = (f32[3,8,32,128]{3,2,1,0:T(8,128)S(1)}, f32[3,8,32,128]{3,2,1,0:T(8,128)}, u32[]{:S(2)}) copy-start(f32[3,8,32,128]{3,2,1,0:T(8,128)} %vel.5) | copy-start | bytes 1179652
  6.0 24.2 %copy-start.21 = (f32[8,32,128]{2,1,0:T(8,128)S(1)}, f32[8,32,128]{2,1,0:T(8,128)}, u32[]{:S(2)}) copy-start(f32[8,32,128]{2,1,0:T(8,128)} %energy.5) | copy-start | bytes 393220
  6.0 24.3 %copy-start.24 = (f32[8,32,128]{2,1,0:T(8,128)S(1)}, f32[8,32,128]{2,1,0:T(8,128)}, u32[]{:S(2)}) copy-start(f32[8,32,128]{2,1,0:T(8,128)} %density.5) | copy-start | bytes 393220
  6.7 27.7 %copy-start.52 = (s32[6]{0:T(128)S(1)}, s32[6]{0:T(128)}, u32[]{:S(2)}) copy-start(s32[6]{0:T(128)} %param.13) | copy-start | bytes 76
  6.7 12.1 %collective-permute-start = (f32[15,32,128]{2,1,0:T(8,128)S(1)}, f32[15,32,128]{2,1,0:T(8,128)S(1)}, u32[]{:S(2)}, u32[]{:S(2)}) collective-permute-start(f32[15,32,128]{2,1,0:T(8,128)S(1)} %get-tuple-element.34), channel_id=1, source_target_pairs={{0,32},{32,64},{64,96},{96,128},{128,160},{160,192},{192,224},{224... | collective-permute-start | bytes 737288 | tf_op jit(solution)/shard_map/ppermute | solution.py:424
  9.2 7.6 %collective-permute-start.1 = (f32[12,32,128]{2,1,0:T(8,128)S(1)}, f32[12,32,128]{2,1,0:T(8,128)S(1)}, u32[]{:S(2)}, u32[]{:S(2)}) collective-permute-start(f32[12,32,128]{2,1,0:T(8,128)S(1)} %get-tuple-element.35), channel_id=1, source_target_pairs={{32,0},{64,32},{96,64},{128,96},{160,128},{192,160},{224,192},{0,2... | collective-permute-start | bytes 589832 | tf_op jit(solution)/shard_map/ppermute | solution.py:425
  18.8 1.0 copy-start.1
  19.8 1.0 copy-start.8
  20.8 0.9 copy-start.20
  21.7 0.9 copy-start.23
  22.7 5.1 %collective-permute-start.2 = (f32[396,128]{1,0:T(8,128)S(1)}, f32[396,128]{1,0:T(8,128)S(1)}, u32[]{:S(2)}, u32[]{:S(2)}) collective-permute-start(f32[396,128]{1,0:T(8,128)S(1)} %get-tuple-element.36), channel_id=1, source_target_pairs={{0,4},{4,8},{8,12},{12,16},{16,20},{20,24},{24,28},{28,0},{1,5},{5... | collective-permute-start | bytes 608264 | tf_op jit(solution)/shard_map/ppermute | solution.py:424
  25.1 5.2 %collective-permute-start.3 = (f32[396,128]{1,0:T(8,128)S(1)}, f32[396,128]{1,0:T(8,128)S(1)}, u32[]{:S(2)}, u32[]{:S(2)}) collective-permute-start(f32[396,128]{1,0:T(8,128)S(1)} %get-tuple-element.37), channel_id=1, source_target_pairs={{4,0},{8,4},{12,8},{16,12},{20,16},{24,20},{28,24},{0,28},{5,1},{9... | collective-permute-start | bytes 608264 | tf_op jit(solution)/shard_map/ppermute | solution.py:425
  31.5 4.9 %collective-permute-start.4 = (f32[128,128]{1,0:T(8,128)S(1)}, f32[128,128]{1,0:T(8,128)S(1)}, u32[]{:S(2)}, u32[]{:S(2)}) collective-permute-start(f32[128,128]{1,0:T(8,128)S(1)} %get-tuple-element.39), channel_id=1, source_target_pairs={{0,1},{1,2},{2,3},{3,0},{4,5},{5,6},{6,7},{7,4},{8,9},{9,10},{10,1... | collective-permute-start | bytes 196616 | tf_op jit(solution)/shard_map/ppermute | solution.py:424
  32.9 3.6 %collective-permute-start.5 = (f32[128,128]{1,0:T(8,128)S(1)}, f32[128,128]{1,0:T(8,128)S(1)}, u32[]{:S(2)}, u32[]{:S(2)}) collective-permute-start(f32[128,128]{1,0:T(8,128)S(1)} %get-tuple-element.40), channel_id=1, source_target_pairs={{1,0},{2,1},{3,2},{0,3},{5,4},{6,5},{7,6},{4,7},{9,8},{10,9},{11,1... | collective-permute-start | bytes 196616 | tf_op jit(solution)/shard_map/ppermute | solution.py:425
  64.1 1.9 %copy-start.5 = (f32[9,9,6,8,256]{4,3,2,1,0:T(8,128)}, f32[9,9,6,8,256]{4,3,2,1,0:T(8,128)S(1)}, u32[]{:S(2)}) copy-start(f32[9,9,6,8,256]{4,3,2,1,0:T(8,128)S(1)} %get-tuple-element.49.terms) | copy-start | bytes 11943940
  66.1 1.2 copy-start.10
  67.2 1.1 copy-start.12
  68.4 1.2 copy-start.14
  69.6 0.7 copy-start.16
  70.3 0.7 copy-start.31
  71.0 0.7 copy-start.33
  71.8 0.7 copy-start.35
  72.5 28.4 %all-to-all-start = ((f32[256,1,128]{2,1,0:T(1,128)}), f32[256,1,128]{2,1,0:T(1,128)S(1)}, u32[]{:S(2)}, u32[]{:S(2)}) async-start(f32[256,1,128]{2,1,0:T(1,128)} %bitcast.4), calls=%async_computation | async-start | bytes 262144 | tf_op jit(solution)/shard_map/all_to_all | solution.py:483
  84.0 2.1 %copy-start.6 = (f32[9,9,6,8,256]{4,3,2,1,0:T(8,128)S(1)}, f32[9,9,6,8,256]{4,3,2,1,0:T(8,128)}, u32[]{:S(2)}) copy-start(f32[9,9,6,8,256]{4,3,2,1,0:T(8,128)} %copy-done.5) | copy-start | bytes 11943940
  86.1 1.0 copy-start.17
  87.1 13.8 %copy-start.11 = (f32[3,12,5,8,256]{4,3,2,1,0:T(8,128)S(1)}, f32[3,12,5,8,256]{4,3,2,1,0:T(8,128)}, u32[]{:S(2)}) copy-start(f32[3,12,5,8,256]{4,3,2,1,0:T(8,128)} %copy-done.10) | copy-start | bytes 4423684
  87.1 13.8 %copy-start.13 = (f32[3,12,5,8,256]{4,3,2,1,0:T(8,128)S(1)}, f32[3,12,5,8,256]{4,3,2,1,0:T(8,128)}, u32[]{:S(2)}) copy-start(f32[3,12,5,8,256]{4,3,2,1,0:T(8,128)} %copy-done.12) | copy-start | bytes 4423684
  88.2 0.8 copy-start.25
  89.0 0.7 copy-start.45
  89.7 9.8 %collective-permute-start.6 = (f32[3,2,5,8,256]{4,3,2,1,0:T(8,128)S(1)}, f32[3,2,5,8,256]{4,3,2,1,0:T(8,128)S(1)}, u32[]{:S(2)}, u32[]{:S(2)}) collective-permute-start(f32[3,2,5,8,256]{4,3,2,1,0:T(8,128)S(1)} %get-tuple-element.50.accel_high), channel_id=1, source_target_pairs={{0,32},{32,64},{64,96},{96,128},{128,160},{160,192},{192,224},{224... | collective-permute-start | bytes 737288 | tf_op jit(solution)/shard_map/ppermute | solution.py:424
  91.1 0.7 copy-start.39
  91.8 8.4 %collective-permute-start.7 = (f32[3,2,5,8,256]{4,3,2,1,0:T(8,128)S(1)}, f32[3,2,5,8,256]{4,3,2,1,0:T(8,128)S(1)}, u32[]{:S(2)}, u32[]{:S(2)}) collective-permute-start(f32[3,2,5,8,256]{4,3,2,1,0:T(8,128)S(1)} %get-tuple-element.51.accel_low), channel_id=1, source_target_pairs={{32,0},{64,32},{96,64},{128,96},{160,128},{192,160},{224,192},{0,2... | collective-permute-start | bytes 737288 | tf_op jit(solution)/shard_map/ppermute | solution.py:425
  94.7 0.7 copy-start.37
  99.5 0.7 copy-start.41
  100.2 0.7 copy-start.43
  100.9 1.4 copy-start.15
  102.3 1.0 copy-start.18
  103.3 1.0 copy-start.26
  104.3 1.0 copy-start.32
  105.3 1.0 copy-start.34
  106.3 1.0 copy-start.36
  107.3 0.9 copy-start.38
  108.2 0.9 copy-start.40
  109.2 0.9 copy-start.42
  110.1 0.9 copy-start.44
  115.2 1.9 %copy-start.3 = (f32[9,9,6,8,256]{4,3,2,1,0:T(8,128)}, f32[9,9,6,8,256]{4,3,2,1,0:T(8,128)S(1)}, u32[]{:S(2)}) copy-start(f32[9,9,6,8,256]{4,3,2,1,0:T(8,128)S(1)} %get-tuple-element.54.terms) | copy-start | bytes 11943940
  117.2 0.8 copy-start.27
  118.0 0.7 copy-start.29
  118.7 0.7 copy-start.47
  119.4 0.7 copy-start.50
  120.0 26.0 %all-to-all-start.1 = ((f32[256,1,128]{2,1,0:T(1,128)}), f32[256,1,128]{2,1,0:T(1,128)S(1)}, u32[]{:S(2)}, u32[]{:S(2)}) async-start(f32[256,1,128]{2,1,0:T(1,128)} %bitcast.14), calls=%async_computation.1 | async-start | bytes 262144 | tf_op jit(solution)/shard_map/all_to_all | solution.py:501
  133.4 2.1 %copy-start.4 = (f32[9,9,6,8,256]{4,3,2,1,0:T(8,128)S(1)}, f32[9,9,6,8,256]{4,3,2,1,0:T(8,128)}, u32[]{:S(2)}) copy-start(f32[9,9,6,8,256]{4,3,2,1,0:T(8,128)} %copy-done.3) | copy-start | bytes 11943940
  135.5 1.0 copy-start.28
  136.5 1.0 copy-start.30
  137.5 0.9 copy-start.46
  138.4 0.9 copy-start.48

commit v2 on v1

v2 whole, which is shorter than its diff:
```python
import functools

import jax
import jax.numpy as jnp
from jax import lax
from jax.experimental import pallas as pl
from jax.experimental.pallas import tpu as pltpu
from jax.sharding import Mesh
from jax.sharding import PartitionSpec as P

GY = ("gy_0", "gy_1")
AXES = ("gx", "gy_0", "gy_1", "gz")

BX, BY, BZ = 8, 32, 128
PX = BX + 4
EX = BX + 1
ROWS = BY + 8
GROUPS = ROWS // 8
LANES = 2 * BZ
SLABS = 6 * PX + 3 * EX
PAIRS = -(-EX // 2)
PACKED = PX + PAIRS
FAR = 1 << 20
ENERGY, DENSITY, GAMMA, WORK = range(4)
MIB = 1 << 20


def next_z(v):
    return pltpu.roll(v, LANES - 1, 1)


def prev_z(v):
    return pltpu.roll(v, 1, 1)


def next_row(v):
    return pltpu.roll(v, 7, 0)


def prev_row(v):
    return pltpu.roll(v, 1, 0)


def slab_ids():
    for field in range(6):
        for plane in range(PX):
            yield field * PX + plane, field, plane
    for field in range(6, 9):
        for plane in range(EX):
            yield 6 * PX + (field - 6) * EX + plane, field, plane


def pack_x(
    gamma_table, disp, vel, energy, density, region,
    up, down, gamma, disp_in, vel_in, energy_in, density_in,
    ids, sems,
):
    moves = ((region, ids), (disp, disp_in), (vel, vel_in), (energy, energy_in), (density, density_in))
    copies = [pltpu.make_async_copy(a, b, sems.at[i]) for i, (a, b) in enumerate(moves)]
    for c in copies:
        c.start()
    copies[0].wait()
    kinds = ids[...]
    value = jnp.zeros(kinds.shape, jnp.float32)
    for r in range(gamma_table.shape[0]):
        value = jnp.where(kinds == r, gamma_table[r], value)
    gamma[...] = value
    up[14] = value[BX - 1]
    for c in copies[1:]:
        c.wait()
    for field in range(6):
        src = disp_in if field < 3 else vel_in
        for p in range(2):
            up[2 * field + p] = src[field % 3, BX - 2 + p]
            down[2 * field + p] = src[field % 3, p]
    up[12] = energy_in[BX - 1]
    up[13] = density_in[BX - 1]


def slab_source(field, plane, disp, vel, energy, density, gamma, x_low, x_high):
    if field < 6:
        if plane < 2:
            return x_low, (2 * field + plane,)
        if plane < BX + 2:
            return (disp if field < 3 else vel), (field % 3, plane - 2)
        return x_high, (2 * field + plane - BX - 2,)
    if plane == 0:
        return x_low, (12 + field - 6,)
    return (energy, density, gamma)[field - 6], (plane - 1,)


def pack_y(disp, vel, energy, density, gamma, x_low, x_high, up, down):
    for k, field, plane in slab_ids():
        ref, at = slab_source(field, plane, disp, vel, energy, density, gamma, x_low, x_high)
        up[4 * k : 4 * k + 4] = ref[(*at, slice(BY - 4, BY))]
        down[4 * k : 4 * k + 4] = ref[(*at, slice(0, 4))]


def pack_z(disp, vel, energy, density, gamma, x_low, x_high, y_low, y_high, main, up, down, stage):
    quad = lax.broadcasted_iota(jnp.int32, (8, BZ), 1) // 4
    for k, field, plane in slab_ids():
        ref, at = slab_source(field, plane, disp, vel, energy, density, gamma, x_low, x_high)
        stage[k, 0:4] = y_low[4 * k : 4 * k + 4]
        stage[k, 4 : BY + 4] = ref[(*at, slice(0, BY))]
        stage[k, BY + 4 : BY + 8] = y_high[4 * k : 4 * k + 4]

    def pack(parts, slot):
        to_up = jnp.zeros((8, BZ), jnp.float32)
        to_down = jnp.zeros((8, BZ), jnp.float32)
        for q, k, j in parts:
            value = stage[k, pl.ds(j, 8, stride=GROUPS), :]
            main[k, j] = value
            to_up = jnp.where(quad == q, pltpu.roll(value, (4 * q + 4) % BZ, 1), to_up)
            here = pltpu.roll(value, 4 * q, 1) if q else value
            to_down = jnp.where(quad == q, here, to_down)
        up[slot] = to_up
        down[slot] = to_down

    def node_plane(plane, carry):
        pack([(f * GROUPS + j, f * PX + plane, j) for f in range(6) for j in range(GROUPS)], plane)
        return carry

    def element_planes(pair, carry, count=2):
        pack(
            [
                ((h * 3 + f) * GROUPS + j, 6 * PX + f * EX + 2 * pair + h, j)
                for h in range(count)
                for f in range(3)
                for j in range(GROUPS)
            ],
            PX + pair,
        )
        return carry

    lax.fori_loop(0, PX, node_plane, 0)
    lax.fori_loop(0, EX // 2, element_planes, 0)
    if EX % 2:
        element_planes(EX // 2, 0, 1)


class Place:
    def __init__(self, where):
        self.x0, self.y0, self.z0 = where[0], where[1], where[2]
        self.nx, self.ny, self.nz = where[3], where[4], where[5]
        self.flag = [where[6 + i] for i in range(6)]
        sublane = lax.broadcasted_iota(jnp.int32, (8, LANES), 0)
        lane = lax.broadcasted_iota(jnp.int32, (8, LANES), 1)
        self.row = GROUPS * sublane + (self.y0 - 4)
        self.col = jnp.where(lane < LANES - BZ // 2, lane, lane - LANES) + self.z0
        inside = (self.col >= 0) & (self.col < self.nz - 1)
        self.row_inside = jnp.where(inside, self.row, -FAR)

    def present(self, plane, j):
        x = self.x0 + plane
        ok = (x >= 0) & (x < self.nx - 1)
        top = jnp.where(ok, self.ny - 1 - j, -2 * FAR)
        return (self.row_inside >= -j) & (self.row_inside < top)

    def counted(self, plane, j):
        x = self.x0 + plane
        ok = (x >= 0) & (x < self.nx - 1)
        top = jnp.where(ok, jnp.minimum(self.ny - 1, self.y0 + BY) - j, -2 * FAR)
        rows = self.row_inside[:, :BZ]
        return (rows >= self.y0 - j) & (rows < top)


def open_factor(flag):
    return jnp.where(flag == 1, 0.0, 1.0)


def strain_pass(fs_d, fd_d, fs_v, fd_v, cof, vol, inv, strain):
    def plane_step(x, carry):
        for j in range(GROUPS):
            grad = []
            for n in range(6):
                f = n % 3
                fs, fd = (fs_d, fd_d) if n < 3 else (fs_v, fd_v)
                a, b = fs[f, x, j], fs[f, x + 1, j]
                c, d = fs[f, x, j + 1], fs[f, x + 1, j + 1]
                p, q = d - a, b - c
                gz = (fd[f, x, j] + fd[f, x + 1, j]) + (fd[f, x, j + 1] + fd[f, x + 1, j + 1])
                grad.append([p + q, p - q, gz])
            m = [[grad[d][e] + 4.0 if d == e else grad[d][e] for e in range(3)] for d in range(3)]
            g = grad[3:]

            def minor(r, s, u, w):
                return m[r][u] * m[s][w] - m[r][w] * m[s][u]

            c = [
                [minor(1, 2, 1, 2), minor(1, 2, 2, 0), minor(1, 2, 0, 1)],
                [minor(2, 0, 1, 2), minor(2, 0, 2, 0), minor(2, 0, 0, 1)],
                [minor(0, 1, 1, 2), minor(0, 1, 2, 0), minor(0, 1, 0, 1)],
            ]
            volume = m[0][0] * c[0][0] + m[0][1] * c[0][1] + m[0][2] * c[0][2]
            change = c[0][0] * g[0][0]
            for d in range(3):
                for e in range(3):
                    if d or e:
                        change = change + c[d][e] * g[d][e]
                    cof[3 * d + e, x, j] = c[d][e]
            inverse = 1.0 / volume
            rate = change * inverse
            vol[x, j] = volume
            inv[x, j] = inverse
            strain[x, j + 1] = rate
            if j == 0:
                strain[x, GROUPS + 1] = next_row(rate)
            if j == GROUPS - 1:
                strain[x, 0] = prev_row(rate)
        return carry

    lax.fori_loop(0, PX - 1, plane_step, 0)


def limited(forward, backward):
    return jnp.maximum(jnp.minimum(forward, backward), 0.0) - jnp.minimum(
        jnp.maximum(forward, backward), 0.0
    )


def stress_pass(place, cof, vol, inv, strain, elems, terms, least, plane_done=None):
    opened = [open_factor(f) for f in place.flag]

    def plane_step(i, low):
        x = i + 1
        gx = place.x0 + i - 1
        for j in range(GROUPS):
            s = strain[x, j + 1]
            back = jnp.where(gx == 0, s * opened[0], s - strain[x - 1, j + 1])
            fore = jnp.where(gx == place.nx - 2, -s * opened[1], strain[x + 1, j + 1] - s)
            rough = limited(fore, back)
            back = jnp.where(place.row == -j, s * opened[2], s - strain[x, j])
            fore = jnp.where(
                place.row == place.ny - 2 - j, -s * opened[3], strain[x, j + 2] - s
            )
            rough = rough + limited(fore, back)
            back = jnp.where(place.col == 0, s * opened[4], s - prev_z(s))
            fore = jnp.where(place.col == place.nz - 2, -s * opened[5], next_z(s) - s)
            rough = rough + limited(fore, back)
            volume = vol[x, j]
            root = jnp.exp(jnp.log(jnp.abs(volume)) * (1.0 / 3.0))
            root = jnp.where(volume < 0.0, -root, root)
            compress = jnp.maximum(-s, 0.0)
            quad = (root * root) * (0.0625 * compress) * (compress + rough)
            g, e = elems[i, GAMMA, j], elems[i, ENERGY, j]
            base = (g - 1.0) * e
            both = base + quad
            ratio = root[:, :BZ] * lax.rsqrt(g[:, :BZ] * base[:, :BZ] + quad[:, :BZ])
            low = jnp.minimum(low, jnp.where(place.counted(i - 1, j), ratio, jnp.inf))
            elems[i, WORK, j] = s * both
            t = elems[i, DENSITY, j] * inv[x, j] * both
            t = jnp.where(place.present(i - 1, j), t, 0.0)
            for d in range(3):
                t0, t1, t2 = t * cof[3 * d, x, j], t * cof[3 * d + 1, x, j], t * cof[3 * d + 2, x, j]
                for n, value in enumerate((t0 + t1, t0 - t1, t2)):
                    terms[3 * d + n, i, j + 1] = value
                    if j == GROUPS - 1:
                        terms[3 * d + n, i, 0] = prev_row(value)
        if plane_done:
            plane_done(i)
        return low

    low = lax.fori_loop(0, EX, plane_step, jnp.full((8, BZ), jnp.inf, jnp.float32))
    low = jnp.broadcast_to(jnp.min(low, axis=0, keepdims=True), (8, BZ))
    for r in range(0, least.shape[0], 8):
        least[r : r + 8] = low


def force_of(terms, d, x, j):
    m, n, t = 3 * d, 3 * d + 1, 3 * d + 2
    r = terms[m, x, j] - terms[n, x + 1, j] + terms[n, x, j + 1] - terms[m, x + 1, j + 1]
    q = (terms[t, x, j] + terms[t, x + 1, j]) + (terms[t, x, j + 1] + terms[t, x + 1, j + 1])
    return (r - q) + prev_z(r + q)


def store_sums(sums, gaps, field, plane, j, both, gap):
    for out, v in ((sums, both), (gaps, gap)):
        out[field, plane, j] = v
        if j == 0:
            out[field, plane, GROUPS] = next_row(v)


def first_step(
    where, main, z_low, z_high,
    nodes_out, elems_out, accel_low, accel_mid, accel_high, unmass_out, least_out,
    fs_d, fd_d, fs_v, fd_v, cof, vol, inv, strain, terms,
    nodes, elems, accel, unmass, least, held, node_sems, elem_sems, sems,
):
    place = Place(where)
    lane = lax.broadcasted_iota(jnp.int32, (8, BZ), 1)

    def extended(k, j, slot, q):
        high, low = z_high[slot], z_low[slot]
        high = pltpu.roll(high, BZ - 4 * q, 1) if q else high
        low = pltpu.roll(low, BZ - 4 - 4 * q, 1) if q < 31 else low
        return jnp.concatenate([main[k, j], jnp.where(lane < BZ // 2, high, low)], axis=1)

    def nodes_copy(plane):
        return pltpu.make_async_copy(nodes.at[plane], nodes_out.at[plane], node_sems.at[plane])

    def elems_copy(i):
        return pltpu.make_async_copy(elems.at[i], elems_out.at[i], elem_sems.at[i])

    def node_plane(plane, carry):
        for field in range(6):
            for j in range(GROUPS):
                value = extended(field * PX + plane, j, plane, field * GROUPS + j)
                nodes[plane, field, j] = value
                after = next_z(value)
                sums, gaps = (fs_d, fd_d) if field < 3 else (fs_v, fd_v)
                store_sums(sums, gaps, field % 3, plane, j, value + after, after - value)
        nodes_copy(plane).start()
        return carry

    def element_planes(pair, carry, count=2):
        for h in range(count):
            for f in range(3):
                for j in range(GROUPS):
                    k = 6 * PX + f * EX + 2 * pair + h
                    value = extended(k, j, PX + pair, (h * 3 + f) * GROUPS + j)
                    elems[2 * pair + h, f, j] = value
        return carry

    lax.fori_loop(0, PX, node_plane, 0)
    lax.fori_loop(0, EX // 2, element_planes, 0)
    if EX % 2:
        element_planes(EX // 2, 0, 1)
    strain_pass(fs_d, fd_d, fs_v, fd_v, cof, vol, inv, strain)
    stress_pass(
        place, cof, vol, inv, strain, elems, terms, least, lambda i: elems_copy(i).start()
    )
    least_copy = pltpu.make_async_copy(least, least_out, sems.at[0])
    least_copy.start()
    copies = [least_copy]
    for i in range(EX):
        for j in range(GROUPS):
            value = jnp.where(place.present(i - 1, j), elems[i, DENSITY, j], 0.0)
            held[i, j + 1] = value
            if j == GROUPS - 1:
                held[i, 0] = prev_row(value)

    def push_plane(x, carry=0):
        for j in range(GROUPS):
            mass = (held[x, j] + held[x + 1, j]) + (held[x, j + 1] + held[x + 1, j + 1])
            mass = 0.125 * (mass + prev_z(mass))
            some = mass > 0.0
            recip = jnp.where(some, 1.0 / jnp.where(some, mass, 1.0), 0.0)
            unmass[x, j] = recip[:, :BZ]
            for d in range(3):
                accel[x, d, j] = force_of(terms, d, x, j) * recip
        return carry

    def send(source, target, n):
        copies.append(pltpu.make_async_copy(source, target, sems.at[n]))
        copies[-1].start()

    lax.fori_loop(0, 2, push_plane, 0)
    send(accel.at[0:2], accel_low, 1)
    lax.fori_loop(BX - 2, BX, push_plane, 0)
    send(accel.at[BX - 2 : BX], accel_high, 2)
    lax.fori_loop(2, BX - 2, push_plane, 0)
    send(accel.at[2 : BX - 2], accel_mid, 3)
    send(unmass, unmass_out, 4)
    for plane in range(PX):
        nodes_copy(plane).wait()
    for i in range(EX):
        elems_copy(i).wait()
    for c in copies:
        c.wait()


def least_of(ref):
    return jnp.min(ref[...])


def second_step(
    where, lows,
    nodes_in, elems_in, unmass_in, got_low, accel_low, accel_mid, accel_high, got_high,
    natural_out, least_out,
    fs_d, fd_d, fs_v, fd_v, cof, vol, inv, strain, terms,
    nodes, elems, accel, unmass, new_vel, natural, stage, least,
    node_sems, accel_sems, plane_sems, sems,
):
    def nodes_copy(x):
        return pltpu.make_async_copy(nodes_in.at[x], nodes.at[x], node_sems.at[x])

    parts, at = [], 0
    for n, source in enumerate((got_low, accel_low, accel_mid, accel_high, got_high)):
        count = source.shape[0]
        copy = pltpu.make_async_copy(source, accel.at[at : at + count], accel_sems.at[n])
        parts.append((at, count, copy))
        at += count
    for first, count, copy in parts:
        copy.start()
        for x in range(first, first + count):
            nodes_copy(x).start()
    elems_copy = pltpu.make_async_copy(elems_in, elems, sems.at[1])
    unmass_copy = pltpu.make_async_copy(unmass_in, unmass, sems.at[2])
    elems_copy.start()
    unmass_copy.start()
    place = Place(where)
    dt = least_of(lows) * 0.0625
    wall = [jnp.where(place.flag[2 * d] == 1, 0, -FAR) for d in range(3)]
    last = (place.nx - 1, place.ny - 1, place.nz - 1)
    edge = [jnp.where(place.flag[2 * d + 1] == 1, last[d], -FAR) for d in range(3)]
    on_z = (place.col == wall[2]) | (place.col == edge[2])

    def move_plane(x, carry):
        nodes_copy(x).wait()
        gx = place.x0 + x - 2
        on_x = (gx == wall[0]) | (gx == edge[0])
        for j in range(GROUPS):
            for d in range(3):
                v = nodes[x, d + 3, j] + dt * accel[x, d, j]
                if d == 0:
                    v = jnp.where(on_x, 0.0, v)
                elif d == 1:
                    v = jnp.where((place.row == wall[1] - j) | (place.row == edge[1] - j), 0.0, v)
                else:
                    v = jnp.where(on_z, 0.0, v)
                new_vel[x, d, j] = v[:, :BZ]
                after = next_z(v)
                store_sums(fs_v, fd_v, d, x, j, v + after, after - v)
                v = nodes[x, d, j] + dt * v
                after = next_z(v)
                store_sums(fs_d, fd_d, d, x, j, v + after, after - v)

        return carry

    for first, count, copy in parts:
        copy.wait()
        lax.fori_loop(first, first + count, move_plane, 0)
    elems_copy.wait()

    def heat_plane(i, carry):
        for j in range(GROUPS):
            e = elems[i, ENERGY, j]
            moved = e - dt * elems[i, WORK, j]
            elems[i, ENERGY, j] = jnp.where(place.present(i - 1, j), moved, e)
        return carry

    lax.fori_loop(0, EX, heat_plane, 0)
    unmass_copy.wait()
    strain_pass(fs_d, fd_d, fs_v, fd_v, cof, vol, inv, strain)
    stress_pass(place, cof, vol, inv, strain, elems, terms, least)
    least_copy = pltpu.make_async_copy(least, least_out, sems.at[0])
    least_copy.start()

    def natural_copy(x):
        return pltpu.make_async_copy(natural.at[x], natural_out.at[x], plane_sems.at[x])

    def push_plane(x, carry):
        for j in range(GROUPS):
            rows = pl.ds(j, 8, stride=GROUPS)
            for d in range(3):
                stage[x, d, rows, :] = force_of(terms, d, x, j)[:, :BZ] * unmass[x, j]
                stage[x, 3 + d, rows, :] = new_vel[x + 2, d, j]
            stage[x, 6, rows, :] = elems[x + 1, ENERGY, j, :, :BZ]
            stage[x, 7, rows, :] = elems[x + 1, WORK, j, :, :BZ]
        for n in range(8):
            natural[x, n] = stage[x, n, 4 : BY + 4, :]
        natural_copy(x).start()
        return carry

    lax.fori_loop(0, BX, push_plane, 0)
    for x in range(BX):
        natural_copy(x).wait()
    least_copy.wait()


def finish(where, lows, again, disp, natural, new_disp, new_vel, new_energy):
    dt = least_of(lows) * 0.0625
    dt2 = least_of(again) * 0.0625
    x0, y0, z0 = where[0], where[1], where[2]
    nx, ny, nz = where[3], where[4], where[5]
    row = lax.broadcasted_iota(jnp.int32, (BY, BZ), 0) + y0
    col = lax.broadcasted_iota(jnp.int32, (BY, BZ), 1) + z0

    def walled(at, low, high, count):
        return ((at == 0) & (where[low] == 1)) | ((at == count - 1) & (where[high] == 1))

    on_y, on_z = walled(row, 8, 9, ny), walled(col, 10, 11, nz)
    inside = (row < ny - 1) & (col < nz - 1)
    for x in range(BX):
        on_x = walled(x0 + x, 6, 7, nx)
        for d in range(3):
            v = natural[x, 3 + d]
            u = jnp.where((on_x, on_y, on_z)[d], 0.0, v + dt2 * natural[x, d])
            new_vel[d, x] = u
            new_disp[d, x] = (disp[d, x] + dt * v) + dt2 * u
        e = natural[x, 6]
        moved = jnp.where(inside, e - dt2 * natural[x, 7], e)
        new_energy[x] = jnp.where(x0 + x < nx - 1, moved, e)


def call(
    kernel, outs, args, smem=0, near=0, scratch=(), limit=48, space=pltpu.VMEM, out_space=pltpu.VMEM
):
    spaces = [pltpu.SMEM] * smem + [pltpu.VMEM] * near
    spaces += [space] * (len(args) - len(spaces))
    specs = [pl.BlockSpec(memory_space=m) for m in spaces]
    pinned = [
        pltpu.with_memory_space_constraint(a, m) if m is pltpu.HBM else a
        for a, m in zip(args, spaces, strict=True)
    ]
    shape = pltpu.HBM if out_space is pltpu.HBM else jax.ShapeDtypeStruct
    return pl.pallas_call(
        kernel,
        out_shape=[shape(s, jnp.float32) for s in outs],
        in_specs=specs,
        out_specs=[pl.BlockSpec(memory_space=out_space) for _ in outs],
        scratch_shapes=[pltpu.VMEM(s, jnp.float32) if isinstance(s, tuple) else s for s in scratch],
        compiler_params=pltpu.CompilerParams(vmem_limit_bytes=limit * MIB),
        name=kernel.__name__,
    )(*pinned)


def swap(up, down, axis):
    size = lax.axis_size(axis)
    ring = [(i, (i + 1) % size) for i in range(size)]
    low = lax.ppermute(up, axis, ring)
    high = lax.ppermute(down, axis, [(b, a) for a, b in ring])
    return low, high


def body(displacement, velocity, energy, density, region, adiabatic, face_flags):
    assert energy.shape == (BX, BY, BZ)
    sizes = (lax.axis_size("gx"), lax.axis_size(GY), lax.axis_size("gz"))
    devices = sizes[0] * sizes[1] * sizes[2]
    where = jnp.stack(
        [
            lax.axis_index("gx") * BX,
            lax.axis_index(GY) * BY,
            lax.axis_index("gz") * BZ,
            jnp.int32(sizes[0] * BX),
            jnp.int32(sizes[1] * BY),
            jnp.int32(sizes[2] * BZ),
        ]
    )
    where = jnp.concatenate([where, face_flags])
    block = (BX, BY, BZ)
    up, down, *own = call(
        pack_x,
        [(15, BY, BZ), (12, BY, BZ), block, (3, *block), (3, *block), block, block],
        (adiabatic, displacement, velocity, energy, density, region),
        smem=1,
        scratch=[pltpu.VMEM(block, jnp.int32), pltpu.SemaphoreType.DMA((5,))],
        limit=2,
        space=pltpu.HBM,
    )
    gamma, *own = own
    x_low, x_high = swap(up, down, "gx")
    own = (*own, gamma, x_low, x_high)
    up, down = call(pack_y, [(4 * SLABS, BZ)] * 2, own, limit=2)
    y_low, y_high = swap(up, down, GY)
    main, up, down = call(
        pack_z,
        [(SLABS, GROUPS, 8, BZ), (PACKED, 8, BZ), (PACKED, 8, BZ)],
        (*own, y_low, y_high),
        scratch=[(SLABS, ROWS, BZ)],
        limit=4,
    )
    z_low, z_high = swap(up, down, "gz")

    chunk = (GROUPS, 8, LANES)
    half = (GROUPS, 8, BZ)
    slots = (GROUPS + 1, 8, LANES)
    passes = [(3, PX, *slots)] * 4 + [
        (9, PX - 1, *chunk),
        (PX - 1, *chunk),
        (PX - 1, *chunk),
        (PX - 1, GROUPS + 2, 8, LANES),
        (9, EX, *slots),
    ]
    sem = pltpu.SemaphoreType.DMA
    nodes, elems, a_low, a_mid, a_high, unmass, least = call(
        first_step,
        [
            (PX, 6, *chunk),
            (EX, 4, *chunk),
            (2, 3, *chunk),
            (BX - 4, 3, *chunk),
            (2, 3, *chunk),
            (BX, *half),
            (devices, BZ),
        ],
        (where, main, z_low, z_high),
        smem=1,
        scratch=[
            *passes,
            (PX, 6, *chunk),
            (EX, 4, *chunk),
            (BX, 3, *chunk),
            (BX, *half),
            (devices, BZ),
            (EX, *slots),
            sem((PX,)),
            sem((EX,)),
            sem((5,)),
        ],
        limit=28,
        out_space=pltpu.HBM,
    )
    lows = lax.all_to_all(least, AXES, 0, 0, tiled=True)
    got_low, got_high = swap(a_high, a_low, "gx")
    natural, least = call(
        second_step,
        [(BX, 8, BY, BZ), (devices, BZ)],
        (where, lows, nodes, elems, unmass, got_low, a_low, a_mid, a_high, got_high),
        smem=1,
        near=1,
        scratch=[
            *passes,
            (PX, 6, *chunk),
            (EX, 4, *chunk),
            (PX, 3, *chunk),
            (BX, *half),
            (PX, 3, *half),
            (BX, 8, BY, BZ),
            (BX, 8, ROWS, BZ),
            (devices, BZ),
            sem((PX,)),
            sem((5,)),
            sem((BX,)),
            sem((3,)),
        ],
        limit=32,
        space=pltpu.HBM,
        out_space=pltpu.HBM,
    )
    again = lax.all_to_all(least, AXES, 0, 0, tiled=True)
    return tuple(
        call(
            finish,
            [(3, *block), (3, *block), block],
            (where, lows, again, displacement, natural),
            smem=1,
            limit=4,
        )
    )


def solution(mesh):
    torus = Mesh(
        mesh.devices.reshape(mesh.shape["gx"], mesh.shape["gy"] // 2, 2, mesh.shape["gz"]), AXES
    )
    nodes, elements = P(None, "gx", GY, "gz"), P("gx", GY, "gz")
    return jax.shard_map(
        body,
        mesh=torus,
        in_specs=(nodes, nodes, elements, elements, elements, P(), P()),
        out_specs=(nodes, nodes, elements),
        check_vma=False,
    )
```

time: 149 us -> 99.6 us (0.67)
  local copies, waits for them, and re-layouts: 45.8 us -> 2.31 us
  blocking collectives: 0 us -> 23.8 us
  Pallas kernels: 37 us -> 23.8 us
  starting transfers between devices: 41 us -> 27.8 us
  waiting for transfers between devices: 23 us -> 21 us
    unnamed x106 -> x12, local copies, waits for them, and re-layouts: 45.7 us -> 2.23 us
    all_to_all x0 -> x1, blocking collectives: none -> 23.8 us  [body(): again = lax.all_to_all(least, AXES, 0, 0, tiled=True)]
    all_to_all x1 -> x0, starting transfers between devices: 13.3 us -> none  [body(): again = lax.all_to_all(least, AXES, 0, 0, tiled=True)]
    pallas_call x8 -> x6, Pallas kernels: 37 us -> 23.8 us  [call(): pl.pallas_call(kernel, out_shape=[shape(s, jnp.float32) for s in outs], i...]
    all_to_all x1 -> x0, waiting for transfers between devices: 6.21 us -> none  [body(): again = lax.all_to_all(least, AXES, 0, 0, tiled=True)]
    ppermute x4, waiting for transfers between devices: 10.8 us -> 14.5 us  [swap(): low = lax.ppermute(up, axis, ring)]
  transfers between devices with their start and end apart: 10 -> 9, of which waited for: 7 -> 7; matrix products, arithmetic and copies ran while one was open for 0% -> 0% of each run, Pallas kernels for 1% -> 0%
where the time goes in v2:
time: 99.6 us; the launch traced here: 99.4 us
  starting transfers between devices  27.8 us (28%)
  Pallas kernels  23.8 us (24%)
  blocking collectives  23.8 us (24%)
  waiting for transfers between devices  21 us (21%)
  local copies, waits for them, and re-layouts  2.31 us (2%)
    all_to_all x1, blocking collectives, body(): again = lax.all_to_all(least, AXES, 0, 0, tiled=True)  23.8 us
    pallas_call x6, Pallas kernels, call(): pl.pallas_call(kernel, out_shape=[shape(s, jnp.float32) for s in outs], i...  23.8 us
    ppermute x4, waiting for transfers between devices, swap(): low = lax.ppermute(up, axis, ring)  14.5 us
    all_to_all x1, starting transfers between devices, body(): lows = lax.all_to_all(least, AXES, 0, 0, tiled=True)  11.5 us
    ppermute x4, starting transfers between devices, swap(): high = lax.ppermute(down, axis, [(b, a) for a, b in ring])  8.47 us
    ppermute x4, starting transfers between devices, swap(): low = lax.ppermute(up, axis, ring)  7.82 us
    ppermute x4, waiting for transfers between devices, swap(): high = lax.ppermute(down, axis, [(b, a) for a, b in ring])  6.07 us
    unnamed x12, local copies, waits for them, and re-layouts  2.23 us
  transfers between devices with their start and end apart: 9, of which 7 were waited for; matrix products, arithmetic and copies ran while one was open for 0% of the time, Pallas kernels for 0%

profile of v2, /device:TPU:1, one launch (start us, length us, event | category | flops | bytes accessed | tf_op | source)
XLA Modules:
  0.0 99.4 jit_solution(9511134684527770313)
XLA Ops:
  0.6 0.0 copy-start.2
  0.6 0.6 copy-done.2
  1.3 1.9 %pack_x.1 = (f32[15,32,128]{2,1,0:T(8,128)S(1)}, f32[12,32,128]{2,1,0:T(8,128)S(1)}, f32[8,32,128]{2,1,0:T(8,128)S(1)}, f32[3,8,32,128]{3,2,1,0:T(8,128)S(1)}, f...) custom-call(f32[11]{0:T(128)S(1)} %copy-done.2, f32[3,8,32,128]{3,2,1,0:T(8,128)} %disp.3, ...), custom_call_target="tpu_custom_call" | custom-call | tf_op jit(solution)/shard_map/pack_x/pallas_call | solution.py:507
  3.2 0.0 copy-start.5
  3.2 2.5 %collective-permute-start = (f32[15,32,128]{2,1,0:T(8,128)S(1)}, f32[15,32,128]{2,1,0:T(8,128)S(1)}, u32[]{:S(2)}, u32[]{:S(2)}) collective-permute-start(f32[15,32,128]{2,1,0:T(8,128)S(1)} %get-tuple-element.29), channel_id=1, source_target_pairs={{0,32},{32,64},{64,96},{96,128},{128,160},{160,192},{192,224},{224... | collective-permute-start | bytes 737288 | tf_op jit(solution)/shard_map/ppermute | solution.py:521
  5.7 4.0 %collective-permute-start.1 = (f32[12,32,128]{2,1,0:T(8,128)S(1)}, f32[12,32,128]{2,1,0:T(8,128)S(1)}, u32[]{:S(2)}, u32[]{:S(2)}) collective-permute-start(f32[12,32,128]{2,1,0:T(8,128)S(1)} %get-tuple-element.30), channel_id=1, source_target_pairs={{32,0},{64,32},{96,64},{128,96},{160,128},{192,160},{224,192},{0,2... | collective-permute-start | bytes 589832 | tf_op jit(solution)/shard_map/ppermute | solution.py:522
  9.7 3.6 %collective-permute-done.1.x_high = f32[12,32,128]{2,1,0:T(8,128)S(1)} collective-permute-done((f32[12,32,128]{2,1,0:T(8,128)S(1)}, f32[12,32,128]{2,1,0:T(8,128)S(1)}, u32[]{:S(2)}, u32[]{:S(2)}) %collective-permute-start.1) | collective-permute-done | bytes 196640 | tf_op jit(solution)/shard_map/ppermute | solution.py:522
  13.3 2.0 %collective-permute-done.x_low = f32[15,32,128]{2,1,0:T(8,128)S(1)} collective-permute-done((f32[15,32,128]{2,1,0:T(8,128)S(1)}, f32[15,32,128]{2,1,0:T(8,128)S(1)}, u32[]{:S(2)}, u32[]{:S(2)}) %collective-permute-start) | collective-permute-done | bytes 245792 | tf_op jit(solution)/shard_map/ppermute | solution.py:521
  15.3 0.1 pack_y.1
  15.4 2.4 %collective-permute-start.2 = (f32[396,128]{1,0:T(8,128)S(1)}, f32[396,128]{1,0:T(8,128)S(1)}, u32[]{:S(2)}, u32[]{:S(2)}) collective-permute-start(f32[396,128]{1,0:T(8,128)S(1)} %get-tuple-element.31), channel_id=1, source_target_pairs={{0,4},{4,8},{8,12},{12,16},{16,20},{20,24},{24,28},{28,0},{1,5},{5... | collective-permute-start | bytes 608264 | tf_op jit(solution)/shard_map/ppermute | solution.py:521
  17.7 0.0 collective-permute-start.3
  17.7 2.7 %collective-permute-done.2.y_low = f32[396,128]{1,0:T(8,128)S(1)} collective-permute-done((f32[396,128]{1,0:T(8,128)S(1)}, f32[396,128]{1,0:T(8,128)S(1)}, u32[]{:S(2)}, u32[]{:S(2)}) %collective-permute-start.2) | collective-permute-done | bytes 202784 | tf_op jit(solution)/shard_map/ppermute | solution.py:521
  20.4 2.5 %collective-permute-done.3.y_high = f32[396,128]{1,0:T(8,128)S(1)} collective-permute-done((f32[396,128]{1,0:T(8,128)S(1)}, f32[396,128]{1,0:T(8,128)S(1)}, u32[]{:S(2)}, u32[]{:S(2)}) %collective-permute-start.3) | collective-permute-done | bytes 202784 | tf_op jit(solution)/shard_map/ppermute | solution.py:522
  22.9 2.4 %pack_z.1 = (f32[99,5,8,128]{3,2,1,0:T(8,128)S(1)}, f32[17,8,128]{2,1,0:T(8,128)S(1)}, f32[17,8,128]{2,1,0:T(8,128)S(1)}) custom-call(f32[3,8,32,128]{3,2,1,0:T(8,128)S(1)} %get-tuple-element.24.disp, f32[3,8,32,128]{3,2,1,0:T(8,128)S(1)} %get-tuple-element.25.vel, f32[8,32,128]{2,1,0:T(8,128)S(1)} %get-tuple-element.26.energy, ...), custom_call_target="tpu_custom_call" | custom-call | tf_op jit(solution)/shard_map/pack_z/pallas_call | solution.py:507
  25.3 1.4 %collective-permute-start.4 = (f32[17,8,128]{2,1,0:T(8,128)S(1)}, f32[17,8,128]{2,1,0:T(8,128)S(1)}, u32[]{:S(2)}, u32[]{:S(2)}) collective-permute-start(f32[17,8,128]{2,1,0:T(8,128)S(1)} %get-tuple-element.34), channel_id=1, source_target_pairs={{0,1},{1,2},{2,3},{3,0},{4,5},{5,6},{6,7},{7,4},{8,9},{9,10},{10,1... | collective-permute-start | bytes 208904 | tf_op jit(solution)/shard_map/ppermute | solution.py:521
  26.7 1.5 %collective-permute-start.5 = (f32[17,8,128]{2,1,0:T(8,128)S(1)}, f32[17,8,128]{2,1,0:T(8,128)S(1)}, u32[]{:S(2)}, u32[]{:S(2)}) collective-permute-start(f32[17,8,128]{2,1,0:T(8,128)S(1)} %get-tuple-element.35), channel_id=1, source_target_pairs={{1,0},{2,1},{3,2},{0,3},{5,4},{6,5},{7,6},{4,7},{9,8},{10,9},{11,1... | collective-permute-start | bytes 208904 | tf_op jit(solution)/shard_map/ppermute | solution.py:522
  28.2 0.0 copy-done.5
  28.2 0.1 concatenate.3.where
  28.3 2.0 %collective-permute-done.4.z_low = f32[17,8,128]{2,1,0:T(8,128)S(1)} collective-permute-done((f32[17,8,128]{2,1,0:T(8,128)S(1)}, f32[17,8,128]{2,1,0:T(8,128)S(1)}, u32[]{:S(2)}, u32[]{:S(2)}) %collective-permute-start.4) | collective-permute-done | bytes 69664 | tf_op jit(solution)/shard_map/ppermute | solution.py:521
  30.3 0.0 collective-permute-done.5.z_high
  30.3 9.2 %first_step.1 = (f32[12,6,5,8,256]{4,3,2,1,0:T(8,128)}, f32[9,4,5,8,256]{4,3,2,1,0:T(8,128)}, f32[2,3,5,8,256]{4,3,2,1,0:T(8,128)}, f32[4,3,5,8,256]{4,3,2,1,0:T...) custom-call(s32[12]{0:T(128)S(1)} %concatenate.3.where, ...), custom_call_target="tpu_custom_call" | custom-call | tf_op jit(solution)/shard_map/first_step/pallas_call | solution.py:507
  39.5 11.5 %all-to-all-start = ((f32[256,1,128]{2,1,0:T(1,128)}), f32[256,1,128]{2,1,0:T(1,128)S(1)}, u32[]{:S(2)}, u32[]{:S(2)}) async-start(f32[256,1,128]{2,1,0:T(1,128)} %bitcast.14), calls=%async_computation | async-start | bytes 262144 | tf_op jit(solution)/shard_map/all_to_all | solution.py:604
  51.0 1.6 %collective-permute-start.6 = (f32[2,3,5,8,256]{4,3,2,1,0:T(8,128)}, f32[2,3,5,8,256]{4,3,2,1,0:T(8,128)S(1)}, u32[]{:S(2)}, u32[]{:S(2)}) collective-permute-start(f32[2,3,5,8,256]{4,3,2,1,0:T(8,128)} %get-tuple-element.40.accel_high), channel_id=1, source_target_pairs={{0,32},{32,64},{64,96},{96,128},{128,160},{160,192},{192,224},{224... | collective-permute-start | bytes 737288 | tf_op jit(solution)/shard_map/ppermute | solution.py:521
  52.6 2.9 %collective-permute-start.7 = (f32[2,3,5,8,256]{4,3,2,1,0:T(8,128)}, f32[2,3,5,8,256]{4,3,2,1,0:T(8,128)S(1)}, u32[]{:S(2)}, u32[]{:S(2)}) collective-permute-start(f32[2,3,5,8,256]{4,3,2,1,0:T(8,128)} %get-tuple-element.41.accel_low), channel_id=1, source_target_pairs={{32,0},{64,32},{96,64},{128,96},{160,128},{192,160},{224,192},{0,2... | collective-permute-start | bytes 737288 | tf_op jit(solution)/shard_map/ppermute | solution.py:522
  55.5 7.7 %collective-permute-done.6.got_low = f32[2,3,5,8,256]{4,3,2,1,0:T(8,128)S(1)} collective-permute-done((f32[2,3,5,8,256]{4,3,2,1,0:T(8,128)}, f32[2,3,5,8,256]{4,3,2,1,0:T(8,128)S(1)}, u32[]{:S(2)}, u32[]{:S(2)}) %collective-permute-start.6) | collective-permute-done | bytes 245792 | tf_op jit(solution)/shard_map/ppermute | solution.py:521
  63.2 0.0 copy-start.3
  63.2 0.0 collective-permute-done.7.got_high
  63.2 0.0 copy-start.4
  63.3 0.5 all-to-all-done
  63.7 0.2 copy-done.3
  63.9 0.1 copy-done.4
  64.0 0.0 copy-start
  64.0 8.6 %second_step.1 = (f32[8,8,32,128]{3,2,1,0:T(8,128)}, f32[256,128]{1,0:T(8,128)}) custom-call(s32[12]{0:T(128)S(1)} %concatenate.3.where, f32[256,128]{1,0:T(8,128)S(1)} %bitcast.11, f32[12,6,5,8,256]{4,3,2,1,0:T(8,128)} %get-tuple-element.37.nodes_in, f32[9,4,5,8,256]{4,3,2,1,0:T(8,128)} %get-tuple-element.38.elems_in, ...), custom_call_target="tpu_custom_call" | custom-call | tf_op jit(solution)/shard_map/second_step/pallas_call | solution.py:507
  72.7 23.8 %all_to_all.22 = f32[256,1,128]{2,1,0:T(1,128)S(1)} all-to-all(f32[256,1,128]{2,1,0:T(1,128)} %bitcast.15), channel_id=1, replica_groups=mesh['gx'=8,'gy_0'=4,'gy_1'=2,'gz'=4] {'gx','gy_0','gy_1','gz'}, dimensions={0} | all-to-all | bytes 262144 | tf_op jit(solution)/shard_map/all_to_all | solution.py:631
  96.5 0.0 copy-done
  96.5 0.0 copy-start.1
  96.5 1.2 %copy-done.1 = f32[8,8,32,128]{3,2,1,0:T(8,128)S(1)} copy-done((f32[8,8,32,128]{3,2,1,0:T(8,128)S(1)}, f32[8,8,32,128]{3,2,1,0:T(8,128)}, u32[]{:S(2)}) %copy-start.1) | copy-done | bytes 1048600
  97.8 1.6 %finish.1 = (f32[3,8,32,128]{3,2,1,0:T(8,128)}, f32[3,8,32,128]{3,2,1,0:T(8,128)}, f32[8,32,128]{2,1,0:T(8,128)}) custom-call(s32[12]{0:T(128)S(1)} %concatenate.3.where, f32[256,128]{1,0:T(8,128)S(1)} %bitcast.12, f32[256,128]{1,0:T(8,128)S(1)} %bitcast.13, f32[3,8,32,128]{3,2,1,0:T(8,128)S(1)} %copy-done, f32[8,8,32,128]{3,2,1,0:T(8,128)S(1)} %copy-done.1), custom_call_target="tpu_custom_call" | custom-call | tf_op jit(solution)/shard_map/finish/pallas_call | solution.py:507
Async XLA Ops:
  0.6 0.7 copy-start.2
  3.2 25.0 %copy-start.5 = (s32[6]{0:T(128)S(1)}, s32[6]{0:T(128)}, u32[]{:S(2)}) copy-start(s32[6]{0:T(128)} %param.13) | copy-start | bytes 76
  3.2 12.1 %collective-permute-start = (f32[15,32,128]{2,1,0:T(8,128)S(1)}, f32[15,32,128]{2,1,0:T(8,128)S(1)}, u32[]{:S(2)}, u32[]{:S(2)}) collective-permute-start(f32[15,32,128]{2,1,0:T(8,128)S(1)} %get-tuple-element.29), channel_id=1, source_target_pairs={{0,32},{32,64},{64,96},{96,128},{128,160},{160,192},{192,224},{224... | collective-permute-start | bytes 737288 | tf_op jit(solution)/shard_map/ppermute | solution.py:521
  5.7 7.6 %collective-permute-start.1 = (f32[12,32,128]{2,1,0:T(8,128)S(1)}, f32[12,32,128]{2,1,0:T(8,128)S(1)}, u32[]{:S(2)}, u32[]{:S(2)}) collective-permute-start(f32[12,32,128]{2,1,0:T(8,128)S(1)} %get-tuple-element.30), channel_id=1, source_target_pairs={{32,0},{64,32},{96,64},{128,96},{160,128},{192,160},{224,192},{0,2... | collective-permute-start | bytes 589832 | tf_op jit(solution)/shard_map/ppermute | solution.py:522
  15.4 5.1 %collective-permute-start.2 = (f32[396,128]{1,0:T(8,128)S(1)}, f32[396,128]{1,0:T(8,128)S(1)}, u32[]{:S(2)}, u32[]{:S(2)}) collective-permute-start(f32[396,128]{1,0:T(8,128)S(1)} %get-tuple-element.31), channel_id=1, source_target_pairs={{0,4},{4,8},{8,12},{12,16},{16,20},{20,24},{24,28},{28,0},{1,5},{5... | collective-permute-start | bytes 608264 | tf_op jit(solution)/shard_map/ppermute | solution.py:521
  17.7 5.2 %collective-permute-start.3 = (f32[396,128]{1,0:T(8,128)S(1)}, f32[396,128]{1,0:T(8,128)S(1)}, u32[]{:S(2)}, u32[]{:S(2)}) collective-permute-start(f32[396,128]{1,0:T(8,128)S(1)} %get-tuple-element.32), channel_id=1, source_target_pairs={{4,0},{8,4},{12,8},{16,12},{20,16},{24,20},{28,24},{0,28},{5,1},{9... | collective-permute-start | bytes 608264 | tf_op jit(solution)/shard_map/ppermute | solution.py:522
  25.3 5.0 %collective-permute-start.4 = (f32[17,8,128]{2,1,0:T(8,128)S(1)}, f32[17,8,128]{2,1,0:T(8,128)S(1)}, u32[]{:S(2)}, u32[]{:S(2)}) collective-permute-start(f32[17,8,128]{2,1,0:T(8,128)S(1)} %get-tuple-element.34), channel_id=1, source_target_pairs={{0,1},{1,2},{2,3},{3,0},{4,5},{5,6},{6,7},{7,4},{8,9},{9,10},{10,1... | collective-permute-start | bytes 208904 | tf_op jit(solution)/shard_map/ppermute | solution.py:521
  26.7 3.7 %collective-permute-start.5 = (f32[17,8,128]{2,1,0:T(8,128)S(1)}, f32[17,8,128]{2,1,0:T(8,128)S(1)}, u32[]{:S(2)}, u32[]{:S(2)}) collective-permute-start(f32[17,8,128]{2,1,0:T(8,128)S(1)} %get-tuple-element.35), channel_id=1, source_target_pairs={{1,0},{2,1},{3,2},{0,3},{5,4},{6,5},{7,6},{4,7},{9,8},{10,9},{11,1... | collective-permute-start | bytes 208904 | tf_op jit(solution)/shard_map/ppermute | solution.py:522
  39.5 24.2 %all-to-all-start = ((f32[256,1,128]{2,1,0:T(1,128)}), f32[256,1,128]{2,1,0:T(1,128)S(1)}, u32[]{:S(2)}, u32[]{:S(2)}) async-start(f32[256,1,128]{2,1,0:T(1,128)} %bitcast.14), calls=%async_computation | async-start | bytes 262144 | tf_op jit(solution)/shard_map/all_to_all | solution.py:604
  51.0 12.2 %collective-permute-start.6 = (f32[2,3,5,8,256]{4,3,2,1,0:T(8,128)}, f32[2,3,5,8,256]{4,3,2,1,0:T(8,128)S(1)}, u32[]{:S(2)}, u32[]{:S(2)}) collective-permute-start(f32[2,3,5,8,256]{4,3,2,1,0:T(8,128)} %get-tuple-element.40.accel_high), channel_id=1, source_target_pairs={{0,32},{32,64},{64,96},{96,128},{128,160},{160,192},{192,224},{224... | collective-permute-start | bytes 737288 | tf_op jit(solution)/shard_map/ppermute | solution.py:521
  52.6 10.7 %collective-permute-start.7 = (f32[2,3,5,8,256]{4,3,2,1,0:T(8,128)}, f32[2,3,5,8,256]{4,3,2,1,0:T(8,128)S(1)}, u32[]{:S(2)}, u32[]{:S(2)}) collective-permute-start(f32[2,3,5,8,256]{4,3,2,1,0:T(8,128)} %get-tuple-element.41.accel_low), channel_id=1, source_target_pairs={{32,0},{64,32},{96,64},{128,96},{160,128},{192,160},{224,192},{0,2... | collective-permute-start | bytes 737288 | tf_op jit(solution)/shard_map/ppermute | solution.py:522
  63.2 0.7 copy-start.3
  63.2 0.8 copy-start.4
  64.0 32.5 %copy-start = (f32[3,8,32,128]{3,2,1,0:T(8,128)S(1)}, f32[3,8,32,128]{3,2,1,0:T(8,128)}, u32[]{:S(2)}) copy-start(f32[3,8,32,128]{3,2,1,0:T(8,128)} %disp.3) | copy-start | bytes 1179652
  96.5 1.2 %copy-start.1 = (f32[8,8,32,128]{3,2,1,0:T(8,128)S(1)}, f32[8,8,32,128]{3,2,1,0:T(8,128)}, u32[]{:S(2)}) copy-start(f32[8,8,32,128]{3,2,1,0:T(8,128)} %get-tuple-element.44.natural) | copy-start | bytes 3145732
